TPU v7x, 128 devices: a whole 4x4x4 slice. The times are simulated.
128 devices in a mesh: shot: 8 (over x_lo, z), gx: 4 (over y), gy: 4 (over x_hi, core).
Axes of the slice: x: 4 (x_hi: 2, x_lo: 2; x = x_hi * 2 + x_lo), y: 4, z: 4, core: 2. Of those that a mesh axis runs over, the one named last changes fastest.
Arguments:
- forward: bfloat16 [8, 2, 9, 16, 512, 512], P('shot', None, None, None, 'gx', 'gy'), may hold values from -6 to 6
- adjoint: bfloat16 [8, 2, 9, 16, 512, 512], P('shot', None, None, None, 'gx', 'gy'), may hold values from -6 to 6
- snap_times: int32 [8, 2], P('shot'), may hold values from 1 to 32, as said below
- sources: int32 [8, 2], P('shot'), may hold values from 0 to 511
- aperture: int32 [8, 4, 4], P('shot', 'gx', 'gy'), may hold values 0 or 1
Outputs:
- smoothed: float32 [3, 16, 512, 512], P(None, 'shot', 'gx', 'gy')
Inputs may be any that keep to these rules, and one draw needn't show every extreme that they name: `snap_times`: each shot's times rise strictly, the first and every step from one to the next being 1 to 16; some shot takes steps of 16 throughout.
All inputs are finite; a program needn't handle non-finite values. No bound on the sum of `aperture` on one device may be relied on, other than what follows from the above.
Results may differ from a plain program's by a relative error of at most 0.0003.
Values sent between devices are 32-bit elements; how exact they have to be, the bound alone decides.
No kernel may reach another device: no remote copies, remote signals or barrier semaphores. Data moves between devices by JAX's collectives and lax.ppermute only.
A program may use at most 64 MiB of HBM per device.

v0:
```python
import jax
import jax.numpy as jnp
from jax import lax
from jax.sharding import PartitionSpec as P

RADIUS = 16
MUTE = 32


spread_x = 0.5
spread_y = 0.375


def in_blocks(x, dim, count):
    before, after = (x.shape[:dim], x.shape[dim + 1 :])
    return jnp.moveaxis(x.reshape(*before, count, -1, *after), dim, 0)


def sent_and_summed(x, axis, dim):
    count = lax.axis_size(axis)
    tiles = lax.all_to_all(in_blocks(x, dim, count), axis, 0, 0, tiled=True)
    return jnp.sum(tiles, axis=0)


def extended(cells, sides, width):
    for axis, dim in sides:
        count = lax.axis_size(axis)
        ends = count - 1
        head = lax.slice_in_dim(cells, 0, width, axis=dim)
        tail = lax.slice_in_dim(cells, cells.shape[dim] - width, cells.shape[dim], axis=dim)
        cells = jnp.concatenate(
            [
                lax.ppermute(tail, axis, [(i, (i + 1) % count) for i in range(ends)]),
                cells,
                lax.ppermute(head, axis, [((i + 1) % count, i) for i in range(ends)]),
            ],
            axis=dim,
        )
    return cells


def band_matrix(count, sigma):
    row_ids = lax.iota(jnp.int32, count)[:, None]
    col_ids = lax.iota(jnp.int32, count + 2 * RADIUS)[None, :]
    offset = col_ids - row_ids - RADIUS
    offset_real = offset.astype(jnp.float32)
    tap_list = jnp.arange(-RADIUS, RADIUS + 1).astype(jnp.float32)
    kernel_sum = jnp.sum(jnp.exp(-tap_list * tap_list / (2.0 * sigma * sigma)))
    values = jnp.exp(-offset_real * offset_real / (2.0 * sigma * sigma)) / kernel_sum
    return jnp.where(jnp.abs(offset) <= RADIUS, values, 0.0)


def on_device(forward, adjoint, snap_times, sources, aperture):
    steps_here = snap_times[0]
    earlier = jnp.concatenate([jnp.zeros((1,), jnp.int32), steps_here[:-1]])
    weights = (steps_here - earlier).astype(jnp.float32) / 8.0
    gradient = None
    for which in range(forward.shape[1]):
        forward_now = forward[0, which]
        adjoint_now = adjoint[0, which]

        def product(comp):
            return forward_now[comp].astype(jnp.float32) * adjoint_now[comp].astype(jnp.float32)

        density_term = product(0) + product(1) + product(2)
        trace_fwd = (
            forward_now[3].astype(jnp.float32)
            + forward_now[4].astype(jnp.float32)
            + forward_now[5].astype(jnp.float32)
        )
        trace_adj = (
            adjoint_now[3].astype(jnp.float32)
            + adjoint_now[4].astype(jnp.float32)
            + adjoint_now[5].astype(jnp.float32)
        )
        lame_term = trace_fwd * trace_adj
        shear_term = 2.0 * (
            product(3) + product(4) + product(5) + 2.0 * (product(6) + product(7) + product(8))
        )
        stacked = jnp.stack([lame_term, shear_term, density_term]) * -weights[which]
        gradient = stacked if gradient is None else gradient + stacked
    width_x = forward.shape[4]
    width_y = forward.shape[5]
    x_cells = lax.axis_index("gx") * width_x + lax.iota(jnp.int32, width_x)
    y_cells = lax.axis_index("gy") * width_y + lax.iota(jnp.int32, width_y)
    delta_x = (x_cells - sources[0, 0]).astype(jnp.float32)
    delta_y = (y_cells - sources[0, 1]).astype(jnp.float32)
    distance = (delta_x * delta_x)[:, None] + (delta_y * delta_y)[None, :]
    taper = (1.0 - jnp.exp(-distance / (2.0 * MUTE * MUTE))) * aperture[0, 0, 0].astype(jnp.float32)
    tapered = gradient * taper
    summed = sent_and_summed(tapered, "shot", 1)
    across_x = band_matrix(width_x, spread_x * RADIUS)
    across_y = band_matrix(width_y, spread_y * RADIUS)
    wide_x = extended(summed, (("gx", 2),), RADIUS)
    smooth_x = jnp.einsum("ij,pljy->pliy", across_x, wide_x, precision=lax.Precision.HIGHEST)
    wide_y = extended(smooth_x, (("gy", 3),), RADIUS)
    return jnp.einsum("zy,pliy->pliz", across_y, wide_y, precision=lax.Precision.HIGHEST)


def solution(mesh):
    in_specs = (
        P("shot", None, None, None, "gx", "gy"),
        P("shot", None, None, None, "gx", "gy"),
        P("shot", None),
        P("shot", None),
        P("shot", "gx", "gy"),
    )
    out_specs = P(None, "shot", "gx", "gy")
    return jax.shard_map(
        on_device, mesh=mesh, in_specs=in_specs, out_specs=out_specs, check_vma=False
    )
```

profile of v0, /device:TPU:1, one launch (start us, length us, event | category | flops | bytes accessed | tf_op | source)
XLA Modules:
  0.0 93.4 jit_solution(9444572764734865174)
XLA Ops:
  0.0 0.0 copy-start
  0.0 4.7 %fusion.8 = (f32[1,1,1,16,128,128]{5,4,3,2,1,0:T(8,128)S(1)}, f32[1,1,1,16,128,128]{5,4,3,2,1,0:T(8,128)S(1)}, f32[1,1,1,16,128,128]{5,4,3,2,1,0:T(8,128)S(1)}) fusion(bf16[1,2,9,16,128,128]{5,4,3,2,1,0:T(8,128)(2,1)} %param.6, bf16[1,2,9,16,128,128]{5,4,3,2,1,0:T(8,128)(2,1)} %param.5), kind=kLoop, calls=%fused_computation.25 | loop fusion | flops 8650752 | bytes 12582912 | tf_op jit(solution)/shard_map/mul | solution.py:76
  4.7 1.8 %copy-done = bf16[1,2,9,16,128,128]{5,4,3,2,1,0:T(8,128)(2,1)S(1)} copy-done((bf16[1,2,9,16,128,128]{5,4,3,2,1,0:T(8,128)(2,1)S(1)}, bf16[1,2,9,16,128,128]{5,4,3,2,1,0:T(8,128)(2,1)}, u32[]{:S(2)}) %copy-start) | copy-done | bytes 9437208
  6.4 4.1 %fusion.12 = (f32[1,1,1,16,128,128]{5,4,3,2,1,0:T(8,128)}, f32[1,1,1,16,128,128]{5,4,3,2,1,0:T(8,128)}) fusion(bf16[1,2,9,16,128,128]{5,4,3,2,1,0:T(8,128)(2,1)S(1)} %copy-done, bf16[1,2,9,16,128,128]{5,4,3,2,1,0:T(8,128)(2,1)} %param.5), kind=kLoop, calls=%fused_computation.29 | loop fusion | flops 9437184 | bytes 11534336 | tf_op jit(solution)/shard_map/mul | solution.py:77
  10.6 0.0 copy-start.1
  10.6 0.0 copy-start.2
  10.6 4.0 %fusion.7 = f32[1,1,1,16,128,128]{5,4,3,2,1,0:T(8,128)} fusion(bf16[1,2,9,16,128,128]{5,4,3,2,1,0:T(8,128)(2,1)S(1)} %copy-done, bf16[1,2,9,16,128,128]{5,4,3,2,1,0:T(8,128)(2,1)} %param.5), kind=kLoop, calls=%fused_computation.24 | loop fusion | flops 6553600 | bytes 7340032 | tf_op jit(solution)/shard_map/mul | solution.py:77
  14.6 0.0 copy-done.1
  14.6 0.6 fusion.59
  15.8 0.0 copy-done.2
  15.8 0.1 fusion.45
  15.9 0.6 fusion.58
  17.8 1.1 %convert_multiply_fusion.6 = (f32[128]{0:T(128)S(1)}, f32[128]{0:T(128)S(1)}) fusion(s32[]{:T(128)} %bitcast.11, s32[]{:T(128)S(6)} %mul.385, s32[]{:T(128)} %bitcast.10, s32[]{:T(128)S(6)} %mul.383), kind=kLoop, calls=%fused_computation.73 | loop fusion | flops 1024 | bytes 1040 | tf_op jit(solution)/shard_map/mul | solution.py:88
  19.0 0.1 subtract_multiply_fusion
  19.1 2.5 %fusion.2 = f32[8,3,2,128,128]{4,3,2,1,0:T(8,128)S(1)} fusion(f32[1,8,2,128,128]{4,3,2,0,1:T(8,128)S(1)} %bitcast.30, f32[1,8,2,128,128]{4,3,2,0,1:T(8,128)} %bitcast.32, f32[1,8,2,128,128]{4,3,2,0,1:T(8,128)S(1)} %bitcast.31, f32[1,8,2,128,128]{4,3,2,0,1:T(8,128)} %bitcast.34, f32[1,8,2,128,128]{4,3,2,0,1:T(8,128)} %bitcast.33, ...), kind=kLoop, calls=%fused_computation.3 | loop fusion | flops 6291456 | bytes 9502728 | tf_op jit(solution)/shard_map/transpose | solution.py:16
  21.6 43.7 %all_to_all.5 = f32[8,3,2,128,128]{4,3,2,1,0:T(8,128)S(1)} all-to-all(f32[8,3,2,128,128]{4,3,2,1,0:T(8,128)S(1)} %fusion.2), channel_id=1, replica_groups=mesh['shot'=8,'gx'=4,'gy'=4] {'shot'}, dimensions={0} | all-to-all | bytes 6291456 | tf_op jit(solution)/shard_map/all_to_all | solution.py:21
  65.3 0.2 reduce_sum.27
  65.5 3.2 %collective-permute-start = (f32[3,2,16,128]{3,2,1,0:T(8,128)S(1)}, f32[3,2,16,128]{3,2,1,0:T(8,128)S(1)}, u32[]{:S(2)}, u32[]{:S(2)}) collective-permute-start(f32[3,2,16,128]{3,2,1,0:T(8,128)S(1)} %get-tuple-element.12), channel_id=1, source_target_pairs={{0,4},{4,8},{8,12},{1,5},{5,9},{9,13},{2,6},{6,10},{10,14},{3,7},{... | collective-permute-start | bytes 147464 | tf_op jit(solution)/shard_map/ppermute | solution.py:33
  68.7 1.3 %collective-permute-start.1 = (f32[3,2,16,128]{3,2,1,0:T(8,128)S(1)}, f32[3,2,16,128]{3,2,1,0:T(8,128)S(1)}, u32[]{:S(2)}, u32[]{:S(2)}) collective-permute-start(f32[3,2,16,128]{3,2,1,0:T(8,128)S(1)} %get-tuple-element.13), channel_id=1, source_target_pairs={{4,0},{8,4},{12,8},{5,1},{9,5},{13,9},{6,2},{10,6},{14,10},{7,3},{... | collective-permute-start | bytes 147464 | tf_op jit(solution)/shard_map/ppermute | solution.py:35
  70.0 0.6 exponential_reduce_fusion.1
  70.6 0.0 collective-permute-done
  70.6 2.9 %collective-permute-done.1 = f32[3,2,16,128]{3,2,1,0:T(8,128)S(1)} collective-permute-done((f32[3,2,16,128]{3,2,1,0:T(8,128)S(1)}, f32[3,2,16,128]{3,2,1,0:T(8,128)S(1)}, u32[]{:S(2)}, u32[]{:S(2)}) %collective-permute-start.1) | collective-permute-done | bytes 49184 | tf_op jit(solution)/shard_map/ppermute | solution.py:35
  73.5 2.1 %convolution_bitcast_fusion = f32[3,2,128,128]{2,3,1,0:T(8,128)S(1)} fusion(f32[3,2,16,128]{3,2,1,0:T(8,128)S(1)} %collective-permute-done.1, f32[3,2,128,128]{3,2,1,0:T(8,128)S(1)} %reduce_sum.27, f32[3,2,16,128]{3,2,1,0:T(8,128)S(1)} %collective-permute-done, f32[]{:T(128)} %exponential_reduce_fusion.1), kind=kOutput, calls=%fused_computation.19 | convolution fusion | flops 189194240 | bytes 884740 | tf_op jit(solution)/shard_map/ij,pljy->pliy/dot_general | solution.py:95
  75.7 8.1 %collective-permute-start.2 = (f32[3,2,128,16]{2,3,1,0:T(8,128)S(1)}, f32[3,2,128,16]{2,3,1,0:T(8,128)S(1)}, u32[]{:S(2)}, u32[]{:S(2)}) collective-permute-start(f32[3,2,128,16]{2,3,1,0:T(8,128)S(1)} %get-tuple-element.10), channel_id=1, source_target_pairs={{0,1},{1,2},{2,3},{4,5},{5,6},{6,7},{8,9},{9,10},{10,11},{12,13},{... | collective-permute-start | bytes 147464 | tf_op jit(solution)/shard_map/ppermute | solution.py:33
  83.7 1.9 %collective-permute-start.3 = (f32[3,2,128,16]{2,3,1,0:T(8,128)S(1)}, f32[3,2,128,16]{2,3,1,0:T(8,128)S(1)}, u32[]{:S(2)}, u32[]{:S(2)}) collective-permute-start(f32[3,2,128,16]{2,3,1,0:T(8,128)S(1)} %get-tuple-element.11), channel_id=1, source_target_pairs={{1,0},{2,1},{3,2},{5,4},{6,5},{7,6},{9,8},{10,9},{11,10},{13,12},{... | collective-permute-start | bytes 147464 | tf_op jit(solution)/shard_map/ppermute | solution.py:35
  85.7 0.6 exponential_reduce_fusion
  86.3 0.0 collective-permute-done.2
  86.3 4.4 %collective-permute-done.3 = f32[3,2,128,16]{2,3,1,0:T(8,128)S(1)} collective-permute-done((f32[3,2,128,16]{2,3,1,0:T(8,128)S(1)}, f32[3,2,128,16]{2,3,1,0:T(8,128)S(1)}, u32[]{:S(2)}, u32[]{:S(2)}) %collective-permute-start.3) | collective-permute-done | bytes 49184 | tf_op jit(solution)/shard_map/ppermute | solution.py:35
  90.7 2.7 %fusion.18 = f32[3,2,128,128]{3,2,1,0:T(8,128)} fusion(f32[3,2,128,16]{2,3,1,0:T(8,128)S(1)} %collective-permute-done.3, f32[3,2,128,128]{2,3,1,0:T(8,128)S(1)} %convolution_bitcast_fusion, f32[3,2,128,16]{2,3,1,0:T(8,128)S(1)} %collective-permute-done.2, f32[]{:T(128)} %exponential_reduce_fusion), kind=kOutput, calls=%fused_computation.37 | convolution fusion | flops 189194240 | bytes 884740 | tf_op jit(solution)/shard_map/zy,pliy->pliz/dot_general | solution.py:97
  (2 shorter events, 0.0 us)
Async XLA Ops:
  0.0 6.4 %copy-start = (bf16[1,2,9,16,128,128]{5,4,3,2,1,0:T(8,128)(2,1)S(1)}, bf16[1,2,9,16,128,128]{5,4,3,2,1,0:T(8,128)(2,1)}, u32[]{:S(2)}) copy-start(bf16[1,2,9,16,128,128]{5,4,3,2,1,0:T(8,128)(2,1)} %param.6) | copy-start | bytes 28311556
  10.6 4.0 %copy-start.1 = (s32[1,2]{1,0:T(1,128)S(1)}, s32[1,2]{1,0:T(1,128)}, u32[]{:S(2)}) copy-start(s32[1,2]{1,0:T(1,128)} %param.8) | copy-start | bytes 28
  10.6 5.2 %copy-start.2 = (s32[1,2]{1,0:T(1,128)S(1)}, s32[1,2]{1,0:T(1,128)}, u32[]{:S(2)}) copy-start(s32[1,2]{1,0:T(1,128)} %param.7) | copy-start | bytes 28
  65.5 5.1 %collective-permute-start = (f32[3,2,16,128]{3,2,1,0:T(8,128)S(1)}, f32[3,2,16,128]{3,2,1,0:T(8,128)S(1)}, u32[]{:S(2)}, u32[]{:S(2)}) collective-permute-start(f32[3,2,16,128]{3,2,1,0:T(8,128)S(1)} %get-tuple-element.12), channel_id=1, source_target_pairs={{0,4},{4,8},{8,12},{1,5},{5,9},{9,13},{2,6},{6,10},{10,14},{3,7},{... | collective-permute-start | bytes 147464 | tf_op jit(solution)/shard_map/ppermute | solution.py:33
  68.7 4.8 %collective-permute-start.1 = (f32[3,2,16,128]{3,2,1,0:T(8,128)S(1)}, f32[3,2,16,128]{3,2,1,0:T(8,128)S(1)}, u32[]{:S(2)}, u32[]{:S(2)}) collective-permute-start(f32[3,2,16,128]{3,2,1,0:T(8,128)S(1)} %get-tuple-element.13), channel_id=1, source_target_pairs={{4,0},{8,4},{12,8},{5,1},{9,5},{13,9},{6,2},{10,6},{14,10},{7,3},{... | collective-permute-start | bytes 147464 | tf_op jit(solution)/shard_map/ppermute | solution.py:35
  75.7 10.6 %collective-permute-start.2 = (f32[3,2,128,16]{2,3,1,0:T(8,128)S(1)}, f32[3,2,128,16]{2,3,1,0:T(8,128)S(1)}, u32[]{:S(2)}, u32[]{:S(2)}) collective-permute-start(f32[3,2,128,16]{2,3,1,0:T(8,128)S(1)} %get-tuple-element.10), channel_id=1, source_target_pairs={{0,1},{1,2},{2,3},{4,5},{5,6},{6,7},{8,9},{9,10},{10,11},{12,13},{... | collective-permute-start | bytes 147464 | tf_op jit(solution)/shard_map/ppermute | solution.py:33
  83.7 6.9 %collective-permute-start.3 = (f32[3,2,128,16]{2,3,1,0:T(8,128)S(1)}, f32[3,2,128,16]{2,3,1,0:T(8,128)S(1)}, u32[]{:S(2)}, u32[]{:S(2)}) collective-permute-start(f32[3,2,128,16]{2,3,1,0:T(8,128)S(1)} %get-tuple-element.11), channel_id=1, source_target_pairs={{1,0},{2,1},{3,2},{5,4},{6,5},{7,6},{9,8},{10,9},{11,10},{13,12},{... | collective-permute-start | bytes 147464 | tf_op jit(solution)/shard_map/ppermute | solution.py:35
where the time goes:
time: 93.7 us; the launch traced here: 93.4 us
  blocking collectives  43.7 us (47%)
  other arithmetic  18 us (19%)
  starting transfers between devices  14.5 us (15%)
  waiting for transfers between devices  7.29 us (8%)
  matrix products  4.83 us (5%)
  local copies, waits for them, and re-layouts  3.03 us (3%)
  between operations  2.04 us (2%)
    all_to_all x1, blocking collectives, sent_and_summed(): tiles = lax.all_to_all(in_blocks(x, dim, count), axis, 0, 0, tiled=True)  43.7 us
    ppermute x2, starting transfers between devices, extended(): lax.ppermute(tail, axis, [(i, (i + 1) % count) for i in range(ends)])  11.3 us
    mul x2, other arithmetic, on_device(): 2.0 * (product(3) + product(4) + product(5) + 2.0 * (product(6) + product...  8.12 us
    ppermute x2, waiting for transfers between devices, extended(): lax.ppermute(head, axis, [((i + 1) % count, i) for i in range(ends)])  7.29 us
    mul x1, other arithmetic, on_device(): lame_term = trace_fwd * trace_adj  4.66 us
    ppermute x2, starting transfers between devices, extended(): lax.ppermute(head, axis, [((i + 1) % count, i) for i in range(ends)])  3.21 us
    dot_general x1, matrix products, on_device(): jnp.einsum('zy,pliy->pliz', across_y, wide_y, precision=lax.Precision.HIG...  2.73 us
    transpose x1, other arithmetic, in_blocks(): return jnp.moveaxis(x.reshape(*before, count, -1, *after), dim, 0)  2.51 us
  transfers between devices with their start and end apart: 4, of which 2 were waited for; matrix products, arithmetic and copies ran while one was open for 1% of the time, Pallas kernels for 0%

commit v1 on v0

v1 whole, which is shorter than its diff:
```python
import functools

import jax
import jax.numpy as jnp
from jax import lax
from jax.experimental import pallas as pl
from jax.experimental.pallas import tpu as pltpu
from jax.sharding import PartitionSpec as P


RADIUS = 16
MUTE = 32
RZ = 4
ROWS = 16

spread_x = 0.5
spread_y = 0.375


def gradient_kernel(steps, n_out, *refs):
    fwd, adj, small = refs[:3]
    outs = refs[3 : 3 + n_out]
    taper, sems, *bufs = refs[3 + n_out :]
    shot = lax.axis_index("shot")
    half, z = lax.div(shot, RZ), lax.rem(shot, RZ)
    copies = []
    for n, (c0, cn, (x, a, b), _) in enumerate(steps):
        lev = 2 * ((half ^ x) * RZ + (z ^ (a ^ (3 * b))))
        copies.append(
            [
                pltpu.make_async_copy(
                    src.at[0, :, pl.ds(c0, cn), pl.ds(lev, 2)], bufs[n].at[i], sems.at[n, i]
                )
                for i, src in enumerate((fwd, adj))
            ]
        )
    for pair in copies:
        for cp in pair:
            cp.start()
    t0, t1 = small[:, 0:1], small[:, 1:2]
    weights = (-(t0.astype(jnp.float32) / 8.0), -((t1 - t0).astype(jnp.float32) / 8.0))
    inside = small[:, 4:5].astype(jnp.float32)
    shape = taper.shape
    xs = lax.broadcasted_iota(jnp.int32, shape, 0) + lax.axis_index("gx") * shape[0]
    ys = lax.broadcasted_iota(jnp.int32, shape, 1) + lax.axis_index("gy") * shape[1]
    dx = (xs - small[:, 2:3]).astype(jnp.float32)
    dy = (ys - small[:, 3:4]).astype(jnp.float32)
    taper[...] = (1.0 - jnp.exp(-(dx * dx + dy * dy) / (2.0 * MUTE * MUTE))) * inside
    for n, (c0, cn, _, where) in enumerate(steps):
        for cp in copies[n]:
            cp.wait()
        buf = bufs[n]

        def body(lev, carry, buf=buf, c0=c0, cn=cn, where=where):
            for r in range(0, shape[0], ROWS):

                def load(i, k, c):
                    return buf[i, k, c, lev, r : r + ROWS, :].astype(jnp.float32)

                def product(k, c):
                    return load(0, k, c) * load(1, k, c)

                sums = None
                for k, w in enumerate(weights):
                    if c0 == 0:
                        terms = [product(k, 0) + product(k, 1) + product(k, 2)]
                    else:
                        f = [load(0, k, c) for c in range(3)]
                        a = [load(1, k, c) for c in range(3)]
                        terms = []
                        if where[0] is not None:
                            terms.append((f[0] + f[1] + f[2]) * (a[0] + a[1] + a[2]))
                        if where[1] is not None:
                            normal = f[0] * a[0] + f[1] * a[1] + f[2] * a[2]
                            cross = product(k, 3) + product(k, 4) + product(k, 5)
                            terms.append(2.0 * (normal + 2.0 * cross))
                    terms = [t * w for t in terms]
                    sums = terms if sums is None else [s + t for s, t in zip(sums, terms)]
                mask = taper[r : r + ROWS, :]
                for s, (o, i) in zip(sums, [p for p in where if p is not None]):
                    outs[o][i, lev, r : r + ROWS, :] = s * mask
            return carry

        lax.fori_loop(0, 2, body, 0)


def gradient(args, steps, counts):
    wx, wy = args[0].shape[4:]
    hbm, vm = pl.BlockSpec(memory_space=pltpu.HBM), pl.BlockSpec(memory_space=pltpu.VMEM)
    return pl.pallas_call(
        functools.partial(gradient_kernel, steps, len(counts)),
        out_shape=[pltpu.VMEM((c, 2, wx, wy), jnp.float32) for c in counts],
        in_specs=[hbm, hbm, vm],
        out_specs=[vm] * len(counts),
        scratch_shapes=[
            pltpu.VMEM((wx, wy), jnp.float32),
            pltpu.SemaphoreType.DMA((len(steps), 2)),
        ]
        + [pltpu.VMEM((2, 2, s[1], 2, wx, wy), jnp.bfloat16) for s in steps],
        compiler_params=pltpu.CompilerParams(vmem_limit_bytes=24 << 20),
    )(*args)


def band(first, rows, cols, sigma):
    offset = (
        first
        + lax.broadcasted_iota(jnp.int32, (rows, cols), 0)
        - lax.broadcasted_iota(jnp.int32, (rows, cols), 1)
    )
    taps = lax.broadcasted_iota(jnp.int32, (8, 128), 1) - RADIUS

    def bell(at):
        real = at.astype(jnp.float32)
        return jnp.where(
            jnp.abs(at) <= RADIUS, jnp.exp(-real * real / (2.0 * sigma * sigma)), 0.0
        )

    return bell(offset) / jnp.sum(bell(taps)[0:1, :], axis=1, keepdims=True)


def across(cells, weights):
    return lax.dot_general(
        cells,
        weights,
        (((0,), (0,)), ((), ())),
        precision=lax.Precision.HIGHEST,
        preferred_element_type=jnp.float32,
    )


def inner_kernel(sigma, cells, out):
    width = cells.shape[1]
    weights = band(0, width, width, sigma)
    for p in range(cells.shape[0]):
        out[p] = across(cells[p], weights)


def outer_kernel(sigma, axis, inner, even_in, odd_in, out):
    width = inner.shape[2]
    at, count = lax.axis_index(axis), lax.axis_size(axis)
    even = lax.rem(at, 2) == 0
    inside = jnp.logical_and(at > 0, at < count - 1)
    before = band(-RADIUS, RADIUS, width, sigma)
    after = band(width, RADIUS, width, sigma)
    first = jnp.where(even, after, before)
    second = jnp.where(inside, jnp.where(even, before, after), 0.0)
    weights = jnp.concatenate([first, second], axis=0)
    for p in range(inner.shape[0]):
        cells = jnp.concatenate([even_in[p], odd_in[p]], axis=0)
        out[p] = inner[p] + across(cells, weights)


def smooth(cells, axis, sigma, last):
    vm = pl.BlockSpec(memory_space=pltpu.VMEM)
    n, r, c = cells.shape
    count = lax.axis_size(axis)
    even = lax.axis_index(axis) % 2 == 0
    head, tail = cells[:, :RADIUS], cells[:, -RADIUS:]
    swaps = [
        [(i, (i + (1 if i % 2 == k else -1)) % count) for i in range(count)] for k in range(2)
    ]
    first = lax.ppermute(jnp.where(even, tail, head), axis, swaps[0])
    second = lax.ppermute(jnp.where(even, head, tail), axis, swaps[1])
    params = pltpu.CompilerParams(vmem_limit_bytes=16 << 20)
    inner = pl.pallas_call(
        functools.partial(inner_kernel, sigma),
        out_shape=pltpu.VMEM((n, c, r), jnp.float32),
        in_specs=[vm],
        out_specs=vm,
        compiler_params=params,
    )(cells)
    return pl.pallas_call(
        functools.partial(outer_kernel, sigma, axis),
        out_shape=(jax.ShapeDtypeStruct if last else pltpu.VMEM)((n, c, r), jnp.float32),
        in_specs=[vm] * 3,
        out_specs=vm,
        compiler_params=params,
    )(inner, first, second)


def on_device(forward, adjoint, snap_times, sources, aperture):
    forward = pltpu.with_memory_space_constraint(forward, pltpu.HBM)
    adjoint = pltpu.with_memory_space_constraint(adjoint, pltpu.HBM)
    small = jnp.concatenate([snap_times, sources, aperture.reshape(1, 1)], axis=1)
    shots = lax.axis_size("shot")
    flips = {"x": RZ, "a": 1, "b": 3}

    def swap(v, dim):
        return lax.ppermute(v, "shot", [(i, i ^ flips[dim]) for i in range(shots)])

    bits = [(p, q) for p in range(2) for q in range(2)]
    lame_1, shear_1, density_1, lame_high = gradient(
        (forward, adjoint, small),
        [(3, 6, (x, 1, 1), ((0, 2 + x), (1, 2 * x + 1))) for x in range(2)]
        + [(3, 6, (x, 0, 1), ((3, x), (1, 2 * x))) for x in range(2)]
        + [(3, 3, (x, 1, 0), ((0, x), None)) for x in range(2)]
        + [(0, 3, (1, a, b), ((2, 2 * a + b),)) for a, b in bits],
        (4, 4, 4, 2),
    )
    shear_1 = swap(shear_1, "b")
    lame_1 = swap(lame_1, "a")
    density_1 = swap(density_1, "x")
    later = lax.optimization_barrier((small, lame_high))[0]
    lame_low, shear_low, shear_high, density_low, density_high = gradient(
        (forward, adjoint, later),
        [(3, 6, (x, 0, 0), ((0, x), (1 + x, 0))) for x in range(2)]
        + [(3, 6, (x, 1, 0), (None, (1 + x, 1))) for x in range(2)]
        + [(0, 3, (0, a, b), ((3 + a, b),)) for a, b in bits],
        (2, 2, 2, 2, 2),
    )

    def finish(first, low, high, dims):
        second = swap(high + first[2:4], dims[0])
        third = swap(low[1] + first[1] + second[1], dims[1])
        return low[0] + first[0] + second[0] + third

    shear = finish(shear_1, shear_low, shear_high, "xa")
    lame = finish(lame_1, lame_low, lame_high, "bx")
    density = finish(density_1, density_low, density_high, "ab")
    cells = jnp.concatenate([lame, shear, density], axis=0)
    along_x = smooth(cells, "gx", spread_x * RADIUS, False)
    smoothed = smooth(along_x, "gy", spread_y * RADIUS, True)
    return smoothed.reshape(3, 2, *smoothed.shape[1:])


def solution(mesh):
    in_specs = (
        P("shot", None, None, None, "gx", "gy"),
        P("shot", None, None, None, "gx", "gy"),
        P("shot", None),
        P("shot", None),
        P("shot", "gx", "gy"),
    )
    out_specs = P(None, "shot", "gx", "gy")
    return jax.shard_map(on_device, mesh=mesh, in_specs=in_specs, out_specs=out_specs, check_vma=False)
```

time: 93.7 us -> 54.5 us (0.58)
  blocking collectives: 43.7 us -> 0 us
  other arithmetic: 18 us -> 1.05 us
  Pallas kernels: 0 us -> 11.4 us
  starting transfers between devices: 14.5 us -> 25.2 us
  waiting for transfers between devices: 7.29 us -> 15.9 us
  matrix products: 4.83 us -> 0 us
  local copies, waits for them, and re-layouts: 3.03 us -> 0 us
  between operations: 2.04 us -> 0.77 us
    all_to_all x1 -> x0, blocking collectives: 43.7 us -> none  [sent_and_summed(): tiles = lax.all_to_all(in_blocks(x, dim, count), axis, 0, 0, tiled=True)]
    mul x5 -> x0, other arithmetic: 14 us -> none  [the longest x2 8.12 us: on_device(): 2.0 * (product(3) + product(4) + product(5) + 2.0 * (product(6) + product...]
    pallas_call x0 -> x6, Pallas kernels: none -> 11.4 us  [the longest x2 8.45 us: gradient(): pl.pallas_call(functools.partial(gradient_kernel, steps, len(counts)), ou...]
    ppermute x4 -> x13, starting transfers between devices: 14.5 us -> 25.2 us  [the longest x9 14.5 us: swap(): return lax.ppermute(v, 'shot', [(i, i ^ flips[dim]) for i in range(shots)])]
    ppermute x4 -> x13, waiting for transfers between devices: 7.29 us -> 15.9 us  [the longest x9 11.8 us: swap(): return lax.ppermute(v, 'shot', [(i, i ^ flips[dim]) for i in range(shots)])]
    dot_general x2 -> x0, matrix products: 4.83 us -> none  [the longest x1 2.73 us: on_device(): jnp.einsum('zy,pliy->pliz', across_y, wide_y, precision=lax.Precision.HIG...]
    transpose x1 -> x0, other arithmetic: 2.51 us -> none  [in_blocks(): return jnp.moveaxis(x.reshape(*before, count, -1, *after), dim, 0)]
    unnamed x6 -> x0, local copies, waits for them, and re-layouts: 1.79 us -> none
  transfers between devices with their start and end apart: 4 -> 13, of which waited for: 2 -> 8; matrix products, arithmetic and copies ran while one was open for 1% -> 0% of each run, Pallas kernels for 0% -> 9%
where the time goes in v1:
time: 54.5 us; the launch traced here: 54.4 us
  starting transfers between devices  25.2 us (46%)
  waiting for transfers between devices  15.9 us (29%)
  Pallas kernels  11.4 us (21%)
  other arithmetic  1.05 us (2%)
  between operations  0.77 us (1%)
    ppermute x9, starting transfers between devices, swap(): return lax.ppermute(v, 'shot', [(i, i ^ flips[dim]) for i in range(shots)])  14.5 us
    ppermute x9, waiting for transfers between devices, swap(): return lax.ppermute(v, 'shot', [(i, i ^ flips[dim]) for i in range(shots)])  11.8 us
    ppermute x2, starting transfers between devices, smooth(): second = lax.ppermute(jnp.where(even, head, tail), axis, swaps[1])  10.8 us
    pallas_call x2, Pallas kernels, gradient(): pl.pallas_call(functools.partial(gradient_kernel, steps, len(counts)), ou...  8.45 us
    ppermute x2, waiting for transfers between devices, smooth(): second = lax.ppermute(jnp.where(even, head, tail), axis, swaps[1])  2.72 us
    pallas_call x2, Pallas kernels, smooth(): pl.pallas_call(functools.partial(outer_kernel, sigma, axis), out_shape=(j...  1.85 us
    ppermute x2, waiting for transfers between devices, smooth(): first = lax.ppermute(jnp.where(even, tail, head), axis, swaps[0])  1.46 us
    pallas_call x2, Pallas kernels, smooth(): pl.pallas_call(functools.partial(inner_kernel, sigma), out_shape=pltpu.VM...  1.11 us
  transfers between devices with their start and end apart: 13, of which 8 were waited for; matrix products, arithmetic and copies ran while one was open for 0% of the time, Pallas kernels for 9%

profile of v1, /device:TPU:1, one launch (start us, length us, event | category | flops | bytes accessed | tf_op | source)
XLA Modules:
  0.0 54.4 jit_solution(17199596694793172696)
XLA Ops:
  0.7 0.7 %pad_add_fusion.refs_2_ = s32[1,5]{1,0:T(1,128)S(1)} fusion(s32[1,1]{1,0:T(1,128)} %bitcast.20, s32[1,2]{1,0:T(1,128)} %param.8, s32[1,2]{1,0:T(1,128)} %param.7), kind=kLoop, calls=%fused_computation.29 | loop fusion | flops 10 | bytes 40 | tf_op jit(solution)/shard_map/concatenate | solution.py:184
  1.4 4.5 %shard_map.55 = (f32[4,2,128,128]{3,2,1,0:T(8,128)S(1)}, f32[4,2,128,128]{3,2,1,0:T(8,128)S(1)}, f32[4,2,128,128]{3,2,1,0:T(8,128)S(1)}, f32[2,2,128,128]{3,2,1,0:T(8,128)S(1)}) custom-call(bf16[1,2,9,16,128,128]{5,4,3,2,1,0:T(8,128)(2,1)} %refs_0_.3, bf16[1,2,9,16,128,128]{5,4,3,2,1,0:T(8,128)(2,1)} %refs_1_.3, s32[1,5]{1,0:T(1,128)S(1)} %pad_add_fusion.refs_2_), custom_call_target="tpu_custom_call" | custom-call | tf_op jit(solution)/shard_map/pallas_call | solution.py:90
  5.9 2.5 %collective-permute-start = (f32[4,2,128,128]{3,2,1,0:T(8,128)S(1)}, f32[4,2,128,128]{3,2,1,0:T(8,128)S(1)}, u32[]{:S(2)}, u32[]{:S(2)}) collective-permute-start(f32[4,2,128,128]{3,2,1,0:T(8,128)S(1)} %get-tuple-element.18), channel_id=1, source_target_pairs={{0,16},{16,0},{32,48},{48,32},{64,80},{80,64},{96,112},{112,96},{1... | collective-permute-start | bytes 1572872 | tf_op jit(solution)/shard_map/ppermute | solution.py:189
  8.4 1.2 %collective-permute-start.6 = (f32[4,2,128,128]{3,2,1,0:T(8,128)S(1)}, f32[4,2,128,128]{3,2,1,0:T(8,128)S(1)}, u32[]{:S(2)}, u32[]{:S(2)}) collective-permute-start(f32[4,2,128,128]{3,2,1,0:T(8,128)S(1)} %get-tuple-element.23), channel_id=1, source_target_pairs={{0,64},{16,80},{32,96},{48,112},{64,0},{80,16},{96,32},{112,48},{1... | collective-permute-start | bytes 1572872 | tf_op jit(solution)/shard_map/ppermute | solution.py:189
  9.6 2.2 %collective-permute-start.3 = (f32[4,2,128,128]{3,2,1,0:T(8,128)S(1)}, f32[4,2,128,128]{3,2,1,0:T(8,128)S(1)}, u32[]{:S(2)}, u32[]{:S(2)}) collective-permute-start(f32[4,2,128,128]{3,2,1,0:T(8,128)S(1)} %get-tuple-element.20), channel_id=1, source_target_pairs={{0,48},{16,32},{32,16},{48,0},{64,112},{80,96},{96,80},{112,64},{1... | collective-permute-start | bytes 1572872 | tf_op jit(solution)/shard_map/ppermute | solution.py:189
  11.9 4.0 %shard_map.56 = (f32[2,2,128,128]{3,2,1,0:T(8,128)S(1)}, f32[2,2,128,128]{3,2,1,0:T(8,128)S(1)}, f32[2,2,128,128]{3,2,1,0:T(8,128)S(1)}, f32[2,2,128,128]{3,2,1,0:T(8,128)S(1)}, f32[2,2,128,128]{3,2,1,0:T(8,128)S(1)}) custom-call(bf16[1,2,9,16,128,128]{5,4,3,2,1,0:T(8,128)(2,1)} %refs_0_.3, bf16[1,2,9,16,128,128]{5,4,3,2,1,0:T(8,128)(2,1)} %refs_1_.3, ...), custom_call_target="tpu_custom_call" | custom-call | tf_op jit(solution)/shard_map/pallas_call | solution.py:90
  15.9 4.2 %collective-permute-done = f32[4,2,128,128]{3,2,1,0:T(8,128)S(1)} collective-permute-done((f32[4,2,128,128]{3,2,1,0:T(8,128)S(1)}, f32[4,2,128,128]{3,2,1,0:T(8,128)S(1)}, u32[]{:S(2)}, u32[]{:S(2)}) %collective-permute-start) | collective-permute-done | bytes 524320 | tf_op jit(solution)/shard_map/ppermute | solution.py:189
  20.1 3.4 %collective-permute-start.1 = (f32[2,2,128,128]{3,2,1,0:T(8,128)S(1)}, f32[2,2,128,128]{3,2,1,0:T(8,128)S(1)}, u32[]{:S(2)}, u32[]{:S(2)}) collective-permute-start(f32[2,2,128,128]{3,2,1,0:T(8,128)S(1)} %slice_add_fusion.2), channel_id=1, source_target_pairs={{0,48},{16,32},{32,16},{48,0},{64,112},{80,96},{96,80},{112,64},{1... | collective-permute-start | bytes 786440 | tf_op jit(solution)/shard_map/ppermute | solution.py:189
  23.5 0.0 collective-permute-done.6
  23.5 0.1 collective-permute-start.7
  23.6 0.0 collective-permute-done.3
  23.6 1.3 %collective-permute-start.4 = (f32[2,2,128,128]{3,2,1,0:T(8,128)S(1)}, f32[2,2,128,128]{3,2,1,0:T(8,128)S(1)}, u32[]{:S(2)}, u32[]{:S(2)}) collective-permute-start(f32[2,2,128,128]{3,2,1,0:T(8,128)S(1)} %slice_add_fusion.1), channel_id=1, source_target_pairs={{0,64},{16,80},{32,96},{48,112},{64,0},{80,16},{96,32},{112,48},{1... | collective-permute-start | bytes 786440 | tf_op jit(solution)/shard_map/ppermute | solution.py:189
  24.9 3.8 %collective-permute-done.1 = f32[2,2,128,128]{3,2,1,0:T(8,128)S(1)} collective-permute-done((f32[2,2,128,128]{3,2,1,0:T(8,128)S(1)}, f32[2,2,128,128]{3,2,1,0:T(8,128)S(1)}, u32[]{:S(2)}, u32[]{:S(2)}) %collective-permute-start.1) | collective-permute-done | bytes 262176 | tf_op jit(solution)/shard_map/ppermute | solution.py:189
  28.8 1.2 %collective-permute-start.2 = (f32[2,128,128]{2,1,0:T(8,128)S(1)}, f32[2,128,128]{2,1,0:T(8,128)S(1)}, u32[]{:S(2)}, u32[]{:S(2)}) collective-permute-start(f32[2,128,128]{2,1,0:T(8,128)S(1)} %fusion.6), channel_id=1, source_target_pairs={{0,64},{16,80},{32,96},{48,112},{64,0},{80,16},{96,32},{112,48},{1... | collective-permute-start | bytes 393224 | tf_op jit(solution)/shard_map/ppermute | solution.py:189
  29.9 0.0 collective-permute-done.7
  30.0 2.5 %collective-permute-start.8 = (f32[2,128,128]{2,1,0:T(8,128)S(1)}, f32[2,128,128]{2,1,0:T(8,128)S(1)}, u32[]{:S(2)}, u32[]{:S(2)}) collective-permute-start(f32[2,128,128]{2,1,0:T(8,128)S(1)} %fusion), channel_id=1, source_target_pairs={{0,48},{16,32},{32,16},{48,0},{64,112},{80,96},{96,80},{112,64},{1... | collective-permute-start | bytes 393224 | tf_op jit(solution)/shard_map/ppermute | solution.py:189
  32.4 0.0 collective-permute-done.4
  32.5 0.1 collective-permute-start.5
  32.6 0.6 %collective-permute-done.2 = f32[2,128,128]{2,1,0:T(8,128)S(1)} collective-permute-done((f32[2,128,128]{2,1,0:T(8,128)S(1)}, f32[2,128,128]{2,1,0:T(8,128)S(1)}, u32[]{:S(2)}, u32[]{:S(2)}) %collective-permute-start.2) | collective-permute-done | bytes 131104 | tf_op jit(solution)/shard_map/ppermute | solution.py:189
  33.2 1.9 %collective-permute-done.8 = f32[2,128,128]{2,1,0:T(8,128)S(1)} collective-permute-done((f32[2,128,128]{2,1,0:T(8,128)S(1)}, f32[2,128,128]{2,1,0:T(8,128)S(1)}, u32[]{:S(2)}, u32[]{:S(2)}) %collective-permute-start.8) | collective-permute-done | bytes 131104 | tf_op jit(solution)/shard_map/ppermute | solution.py:189
  35.1 1.3 %collective-permute-done.5 = f32[2,128,128]{2,1,0:T(8,128)S(1)} collective-permute-done((f32[2,128,128]{2,1,0:T(8,128)S(1)}, f32[2,128,128]{2,1,0:T(8,128)S(1)}, u32[]{:S(2)}, u32[]{:S(2)}) %collective-permute-start.5) | collective-permute-done | bytes 131104 | tf_op jit(solution)/shard_map/ppermute | solution.py:189
  36.4 2.8 %collective-permute-start.10 = (f32[6,16,128]{2,1,0:T(8,128)S(1)}, f32[6,16,128]{2,1,0:T(8,128)S(1)}, u32[]{:S(2)}, u32[]{:S(2)}) collective-permute-start(f32[6,16,128]{2,1,0:T(8,128)S(1)} %get-tuple-element.27), channel_id=1, source_target_pairs={{0,12},{4,8},{8,4},{12,0},{1,13},{5,9},{9,5},{13,1},{2,14},{6,10},... | collective-permute-start | bytes 147464 | tf_op jit(solution)/shard_map/ppermute | solution.py:163
  39.3 0.0 collective-permute-start.9
  39.3 0.6 %shard_map.57.inner = f32[6,128,128]{2,1,0:T(8,128)S(1)} custom-call(f32[6,128,128]{2,1,0:T(8,128)S(1)} %pad_maximum_fusion.cells), custom_call_target="tpu_custom_call" | custom-call | tf_op jit(solution)/shard_map/pallas_call | solution.py:165
  39.8 0.9 %collective-permute-done.10.odd_in = f32[6,16,128]{2,1,0:T(8,128)S(1)} collective-permute-done((f32[6,16,128]{2,1,0:T(8,128)S(1)}, f32[6,16,128]{2,1,0:T(8,128)S(1)}, u32[]{:S(2)}, u32[]{:S(2)}) %collective-permute-start.10) | collective-permute-done | bytes 49184 | tf_op jit(solution)/shard_map/ppermute | solution.py:163
  40.7 1.5 %collective-permute-done.9.even_in = f32[6,16,128]{2,1,0:T(8,128)S(1)} collective-permute-done((f32[6,16,128]{2,1,0:T(8,128)S(1)}, f32[6,16,128]{2,1,0:T(8,128)S(1)}, u32[]{:S(2)}, u32[]{:S(2)}) %collective-permute-start.9) | collective-permute-done | bytes 49184 | tf_op jit(solution)/shard_map/ppermute | solution.py:162
  42.2 0.6 %shard_map.58.cells = f32[6,128,128]{2,1,0:T(8,128)S(1)} custom-call(f32[6,128,128]{2,1,0:T(8,128)S(1)} %shard_map.57.inner, f32[6,16,128]{2,1,0:T(8,128)S(1)} %collective-permute-done.9.even_in, f32[6,16,128]{2,1,0:T(8,128)S(1)} %collective-permute-done.10.odd_in), custom_call_target="tpu_custom_call" | custom-call | tf_op jit(solution)/shard_map/pallas_call | solution.py:172
  42.8 7.9 %collective-permute-start.12 = (f32[6,16,128]{2,1,0:T(8,128)S(1)}, f32[6,16,128]{2,1,0:T(8,128)S(1)}, u32[]{:S(2)}, u32[]{:S(2)}) collective-permute-start(f32[6,16,128]{2,1,0:T(8,128)S(1)} %get-tuple-element.25), channel_id=1, source_target_pairs={{0,3},{1,2},{2,1},{3,0},{4,7},{5,6},{6,5},{7,4},{8,11},{9,10},{10,... | collective-permute-start | bytes 147464 | tf_op jit(solution)/shard_map/ppermute | solution.py:163
  50.7 0.0 collective-permute-start.11
  50.7 0.6 %shard_map.59.inner = f32[6,128,128]{2,1,0:T(8,128)S(1)} custom-call(f32[6,128,128]{2,1,0:T(8,128)S(1)} %shard_map.58.cells), custom_call_target="tpu_custom_call" | custom-call | tf_op jit(solution)/shard_map/pallas_call | solution.py:165
  51.3 1.8 %collective-permute-done.12.odd_in = f32[6,16,128]{2,1,0:T(8,128)S(1)} collective-permute-done((f32[6,16,128]{2,1,0:T(8,128)S(1)}, f32[6,16,128]{2,1,0:T(8,128)S(1)}, u32[]{:S(2)}, u32[]{:S(2)}) %collective-permute-start.12) | collective-permute-done | bytes 49184 | tf_op jit(solution)/shard_map/ppermute | solution.py:163
  53.1 0.0 collective-permute-done.11.even_in
  53.1 1.3 %shard_map.60 = f32[6,128,128]{2,1,0:T(8,128)} custom-call(f32[6,128,128]{2,1,0:T(8,128)S(1)} %shard_map.59.inner, f32[6,16,128]{2,1,0:T(8,128)S(1)} %collective-permute-done.11.even_in, f32[6,16,128]{2,1,0:T(8,128)S(1)} %collective-permute-done.12.odd_in), custom_call_target="tpu_custom_call" | custom-call | tf_op jit(solution)/shard_map/pallas_call | solution.py:172
  (12 shorter events, 0.3 us)
Async XLA Ops:
  5.9 14.2 %collective-permute-start = (f32[4,2,128,128]{3,2,1,0:T(8,128)S(1)}, f32[4,2,128,128]{3,2,1,0:T(8,128)S(1)}, u32[]{:S(2)}, u32[]{:S(2)}) collective-permute-start(f32[4,2,128,128]{3,2,1,0:T(8,128)S(1)} %get-tuple-element.18), channel_id=1, source_target_pairs={{0,16},{16,0},{32,48},{48,32},{64,80},{80,64},{96,112},{112,96},{1... | collective-permute-start | bytes 1572872 | tf_op jit(solution)/shard_map/ppermute | solution.py:189
  8.4 15.1 %collective-permute-start.6 = (f32[4,2,128,128]{3,2,1,0:T(8,128)S(1)}, f32[4,2,128,128]{3,2,1,0:T(8,128)S(1)}, u32[]{:S(2)}, u32[]{:S(2)}) collective-permute-start(f32[4,2,128,128]{3,2,1,0:T(8,128)S(1)} %get-tuple-element.23), channel_id=1, source_target_pairs={{0,64},{16,80},{32,96},{48,112},{64,0},{80,16},{96,32},{112,48},{1... | collective-permute-start | bytes 1572872 | tf_op jit(solution)/shard_map/ppermute | solution.py:189
  9.6 14.0 %collective-permute-start.3 = (f32[4,2,128,128]{3,2,1,0:T(8,128)S(1)}, f32[4,2,128,128]{3,2,1,0:T(8,128)S(1)}, u32[]{:S(2)}, u32[]{:S(2)}) collective-permute-start(f32[4,2,128,128]{3,2,1,0:T(8,128)S(1)} %get-tuple-element.20), channel_id=1, source_target_pairs={{0,48},{16,32},{32,16},{48,0},{64,112},{80,96},{96,80},{112,64},{1... | collective-permute-start | bytes 1572872 | tf_op jit(solution)/shard_map/ppermute | solution.py:189
  20.1 8.7 %collective-permute-start.1 = (f32[2,2,128,128]{3,2,1,0:T(8,128)S(1)}, f32[2,2,128,128]{3,2,1,0:T(8,128)S(1)}, u32[]{:S(2)}, u32[]{:S(2)}) collective-permute-start(f32[2,2,128,128]{3,2,1,0:T(8,128)S(1)} %slice_add_fusion.2), channel_id=1, source_target_pairs={{0,48},{16,32},{32,16},{48,0},{64,112},{80,96},{96,80},{112,64},{1... | collective-permute-start | bytes 786440 | tf_op jit(solution)/shard_map/ppermute | solution.py:189
  23.5 6.4 %collective-permute-start.7 = (f32[2,2,128,128]{3,2,1,0:T(8,128)S(1)}, f32[2,2,128,128]{3,2,1,0:T(8,128)S(1)}, u32[]{:S(2)}, u32[]{:S(2)}) collective-permute-start(f32[2,2,128,128]{3,2,1,0:T(8,128)S(1)} %slice_add_fusion), channel_id=1, source_target_pairs={{0,16},{16,0},{32,48},{48,32},{64,80},{80,64},{96,112},{112,96},{1... | collective-permute-start | bytes 786440 | tf_op jit(solution)/shard_map/ppermute | solution.py:189
  23.6 8.8 %collective-permute-start.4 = (f32[2,2,128,128]{3,2,1,0:T(8,128)S(1)}, f32[2,2,128,128]{3,2,1,0:T(8,128)S(1)}, u32[]{:S(2)}, u32[]{:S(2)}) collective-permute-start(f32[2,2,128,128]{3,2,1,0:T(8,128)S(1)} %slice_add_fusion.1), channel_id=1, source_target_pairs={{0,64},{16,80},{32,96},{48,112},{64,0},{80,16},{96,32},{112,48},{1... | collective-permute-start | bytes 786440 | tf_op jit(solution)/shard_map/ppermute | solution.py:189
  28.8 4.4 %collective-permute-start.2 = (f32[2,128,128]{2,1,0:T(8,128)S(1)}, f32[2,128,128]{2,1,0:T(8,128)S(1)}, u32[]{:S(2)}, u32[]{:S(2)}) collective-permute-start(f32[2,128,128]{2,1,0:T(8,128)S(1)} %fusion.6), channel_id=1, source_target_pairs={{0,64},{16,80},{32,96},{48,112},{64,0},{80,16},{96,32},{112,48},{1... | collective-permute-start | bytes 393224 | tf_op jit(solution)/shard_map/ppermute | solution.py:189
  30.0 5.1 %collective-permute-start.8 = (f32[2,128,128]{2,1,0:T(8,128)S(1)}, f32[2,128,128]{2,1,0:T(8,128)S(1)}, u32[]{:S(2)}, u32[]{:S(2)}) collective-permute-start(f32[2,128,128]{2,1,0:T(8,128)S(1)} %fusion), channel_id=1, source_target_pairs={{0,48},{16,32},{32,16},{48,0},{64,112},{80,96},{96,80},{112,64},{1... | collective-permute-start | bytes 393224 | tf_op jit(solution)/shard_map/ppermute | solution.py:189
  32.5 3.9 %collective-permute-start.5 = (f32[2,128,128]{2,1,0:T(8,128)S(1)}, f32[2,128,128]{2,1,0:T(8,128)S(1)}, u32[]{:S(2)}, u32[]{:S(2)}) collective-permute-start(f32[2,128,128]{2,1,0:T(8,128)S(1)} %fusion.3), channel_id=1, source_target_pairs={{0,16},{16,0},{32,48},{48,32},{64,80},{80,64},{96,112},{112,96},{1... | collective-permute-start | bytes 393224 | tf_op jit(solution)/shard_map/ppermute | solution.py:189
  36.4 4.3 %collective-permute-start.10 = (f32[6,16,128]{2,1,0:T(8,128)S(1)}, f32[6,16,128]{2,1,0:T(8,128)S(1)}, u32[]{:S(2)}, u32[]{:S(2)}) collective-permute-start(f32[6,16,128]{2,1,0:T(8,128)S(1)} %get-tuple-element.27), channel_id=1, source_target_pairs={{0,12},{4,8},{8,4},{12,0},{1,13},{5,9},{9,5},{13,1},{2,14},{6,10},... | collective-permute-start | bytes 147464 | tf_op jit(solution)/shard_map/ppermute | solution.py:163
  39.3 2.9 %collective-permute-start.9 = (f32[6,16,128]{2,1,0:T(8,128)S(1)}, f32[6,16,128]{2,1,0:T(8,128)S(1)}, u32[]{:S(2)}, u32[]{:S(2)}) collective-permute-start(f32[6,16,128]{2,1,0:T(8,128)S(1)} %get-tuple-element.28), channel_id=1, source_target_pairs={{0,4},{4,0},{8,12},{12,8},{1,5},{5,1},{9,13},{13,9},{2,6},{6,2},{1... | collective-permute-start | bytes 147464 | tf_op jit(solution)/shard_map/ppermute | solution.py:162
  42.8 10.3 %collective-permute-start.12 = (f32[6,16,128]{2,1,0:T(8,128)S(1)}, f32[6,16,128]{2,1,0:T(8,128)S(1)}, u32[]{:S(2)}, u32[]{:S(2)}) collective-permute-start(f32[6,16,128]{2,1,0:T(8,128)S(1)} %get-tuple-element.25), channel_id=1, source_target_pairs={{0,3},{1,2},{2,1},{3,0},{4,7},{5,6},{6,5},{7,4},{8,11},{9,10},{10,... | collective-permute-start | bytes 147464 | tf_op jit(solution)/shard_map/ppermute | solution.py:163
  50.7 2.4 %collective-permute-start.11 = (f32[6,16,128]{2,1,0:T(8,128)S(1)}, f32[6,16,128]{2,1,0:T(8,128)S(1)}, u32[]{:S(2)}, u32[]{:S(2)}) collective-permute-start(f32[6,16,128]{2,1,0:T(8,128)S(1)} %get-tuple-element.26), channel_id=1, source_target_pairs={{0,1},{1,0},{2,3},{3,2},{4,5},{5,4},{6,7},{7,6},{8,9},{9,8},{10,11... | collective-permute-start | bytes 147464 | tf_op jit(solution)/shard_map/ppermute | solution.py:162

commit v2 on v1

--- a/solution.py
+++ b/solution.py
@@ -17,10 +17,11 @@
 spread_y = 0.375
 
 
-def gradient_kernel(steps, n_out, *refs):
+def gradient_kernel(steps, n_out, carried, *refs):
     fwd, adj, small = refs[:3]
-    outs = refs[3 : 3 + n_out]
-    taper, sems, *bufs = refs[3 + n_out :]
+    whole = refs[3 : 3 + len(carried)]
+    outs = refs[3 + len(carried) :][:n_out]
+    taper, sems, *bufs = refs[3 + len(carried) + n_out :]
     shot = lax.axis_index("shot")
     half, z = lax.div(shot, RZ), lax.rem(shot, RZ)
     copies = []
@@ -37,14 +38,17 @@
     for pair in copies:
         for cp in pair:
             cp.start()
-    t0, t1 = small[:, 0:1], small[:, 1:2]
+    for src, (o, i) in zip(whole, carried):
+        outs[o][i] = src[0]
+    times_etc = small[0]
+    t0, t1 = times_etc[:, 0:1], times_etc[:, 1:2]
     weights = (-(t0.astype(jnp.float32) / 8.0), -((t1 - t0).astype(jnp.float32) / 8.0))
-    inside = small[:, 4:5].astype(jnp.float32)
+    inside = times_etc[:, 4:5].astype(jnp.float32)
     shape = taper.shape
     xs = lax.broadcasted_iota(jnp.int32, shape, 0) + lax.axis_index("gx") * shape[0]
     ys = lax.broadcasted_iota(jnp.int32, shape, 1) + lax.axis_index("gy") * shape[1]
-    dx = (xs - small[:, 2:3]).astype(jnp.float32)
-    dy = (ys - small[:, 3:4]).astype(jnp.float32)
+    dx = (xs - times_etc[:, 2:3]).astype(jnp.float32)
+    dy = (ys - times_etc[:, 3:4]).astype(jnp.float32)
     taper[...] = (1.0 - jnp.exp(-(dx * dx + dy * dy) / (2.0 * MUTE * MUTE))) * inside
     for n, (c0, cn, _, where) in enumerate(steps):
         for cp in copies[n]:
@@ -84,21 +88,29 @@
         lax.fori_loop(0, 2, body, 0)
 
 
-def gradient(args, steps, counts):
+def gradient(args, steps, carried, counts):
+    names = list(counts)
+
+    def place(where):
+        return None if where is None else (names.index(where[0]), where[1])
+
+    steps = [(*step[:3], tuple(place(w) for w in step[3])) for step in steps]
+    kept = [place(where) for _, where in carried]
     wx, wy = args[0].shape[4:]
     hbm, vm = pl.BlockSpec(memory_space=pltpu.HBM), pl.BlockSpec(memory_space=pltpu.VMEM)
-    return pl.pallas_call(
-        functools.partial(gradient_kernel, steps, len(counts)),
-        out_shape=[pltpu.VMEM((c, 2, wx, wy), jnp.float32) for c in counts],
-        in_specs=[hbm, hbm, vm],
-        out_specs=[vm] * len(counts),
+    outs = pl.pallas_call(
+        functools.partial(gradient_kernel, steps, len(names), kept),
+        out_shape=[pltpu.VMEM((c, 2, wx, wy), jnp.float32) for c in counts.values()],
+        in_specs=[hbm, hbm] + [vm] * (1 + len(kept)),
+        out_specs=[vm] * len(names),
         scratch_shapes=[
             pltpu.VMEM((wx, wy), jnp.float32),
             pltpu.SemaphoreType.DMA((len(steps), 2)),
         ]
         + [pltpu.VMEM((2, 2, s[1], 2, wx, wy), jnp.bfloat16) for s in steps],
-        compiler_params=pltpu.CompilerParams(vmem_limit_bytes=24 << 20),
-    )(*args)
+        compiler_params=pltpu.CompilerParams(vmem_limit_bytes=12 << 20),
+    )(*args, *(src for src, _ in carried))
+    return dict(zip(names, outs))
 
 
 def band(first, rows, cols, sigma):
@@ -118,25 +130,26 @@
     return bell(offset) / jnp.sum(bell(taps)[0:1, :], axis=1, keepdims=True)
 
 
+def three_parts(values, order):
+    high = values.astype(jnp.bfloat16)
+    low = (values - high.astype(jnp.float32)).astype(jnp.bfloat16)
+    return jnp.concatenate([low if part else high for part in order], axis=0)
+
+
 def across(cells, weights):
     return lax.dot_general(
-        cells,
+        three_parts(cells, (0, 0, 1)),
         weights,
         (((0,), (0,)), ((), ())),
-        precision=lax.Precision.HIGHEST,
         preferred_element_type=jnp.float32,
     )
 
 
-def inner_kernel(sigma, cells, out):
+def inner_kernel(sigma, axis, cells, out, halo_weights):
     width = cells.shape[1]
-    weights = band(0, width, width, sigma)
+    weights = three_parts(band(0, width, width, sigma), (0, 1, 0))
     for p in range(cells.shape[0]):
         out[p] = across(cells[p], weights)
-
-
-def outer_kernel(sigma, axis, inner, even_in, odd_in, out):
-    width = inner.shape[2]
     at, count = lax.axis_index(axis), lax.axis_size(axis)
     even = lax.rem(at, 2) == 0
     inside = jnp.logical_and(at > 0, at < count - 1)
@@ -144,10 +157,13 @@
     after = band(width, RADIUS, width, sigma)
     first = jnp.where(even, after, before)
     second = jnp.where(inside, jnp.where(even, before, after), 0.0)
-    weights = jnp.concatenate([first, second], axis=0)
+    halo_weights[...] = three_parts(jnp.concatenate([first, second], axis=0), (0, 1, 0))
+
+
+def outer_kernel(inner, weights, even_in, odd_in, out):
     for p in range(inner.shape[0]):
         cells = jnp.concatenate([even_in[p], odd_in[p]], axis=0)
-        out[p] = inner[p] + across(cells, weights)
+        out[p] = inner[p] + across(cells, weights[...])
 
 
 def smooth(cells, axis, sigma, last):
@@ -162,61 +178,116 @@
     first = lax.ppermute(jnp.where(even, tail, head), axis, swaps[0])
     second = lax.ppermute(jnp.where(even, head, tail), axis, swaps[1])
     params = pltpu.CompilerParams(vmem_limit_bytes=16 << 20)
-    inner = pl.pallas_call(
-        functools.partial(inner_kernel, sigma),
-        out_shape=pltpu.VMEM((n, c, r), jnp.float32),
+    inner, weights = pl.pallas_call(
+        functools.partial(inner_kernel, sigma, axis),
+        out_shape=[
+            pltpu.VMEM((n, c, r), jnp.float32),
+            pltpu.VMEM((6 * RADIUS, r), jnp.bfloat16),
+        ],
         in_specs=[vm],
-        out_specs=vm,
+        out_specs=[vm] * 2,
         compiler_params=params,
     )(cells)
     return pl.pallas_call(
-        functools.partial(outer_kernel, sigma, axis),
+        outer_kernel,
         out_shape=(jax.ShapeDtypeStruct if last else pltpu.VMEM)((n, c, r), jnp.float32),
-        in_specs=[vm] * 3,
+        in_specs=[vm] * 4,
         out_specs=vm,
         compiler_params=params,
-    )(inner, first, second)
+    )(inner, weights, first, second)
+
+
+def add_up_kernel(mine_1, mine_0, in10, in01_1, sent, rest):
+    sent[...] = mine_1[0] + in10[1] + in01_1[...]
+    rest[...] = mine_0[0] + in10[0]
+
+
+def add_up(mine_1, mine_0, in10, in01_1):
+    vm = pl.BlockSpec(memory_space=pltpu.VMEM)
+    return pl.pallas_call(
+        add_up_kernel,
+        out_shape=[pltpu.VMEM(in01_1.shape, jnp.float32)] * 2,
+        in_specs=[vm] * 4,
+        out_specs=[vm] * 2,
+        compiler_params=pltpu.CompilerParams(vmem_limit_bytes=4 << 20),
+        name="add_up",
+    )(mine_1, mine_0, pltpu.with_memory_space_constraint(in10, pltpu.VMEM), in01_1)
 
 
 def on_device(forward, adjoint, snap_times, sources, aperture):
     forward = pltpu.with_memory_space_constraint(forward, pltpu.HBM)
     adjoint = pltpu.with_memory_space_constraint(adjoint, pltpu.HBM)
-    small = jnp.concatenate([snap_times, sources, aperture.reshape(1, 1)], axis=1)
+    small = jnp.concatenate([snap_times[None], sources[None], aperture], axis=2)
     shots = lax.axis_size("shot")
     flips = {"x": RZ, "a": 1, "b": 3}
 
     def swap(v, dim):
         return lax.ppermute(v, "shot", [(i, i ^ flips[dim]) for i in range(shots)])
 
-    bits = [(p, q) for p in range(2) for q in range(2)]
-    lame_1, shear_1, density_1, lame_high = gradient(
-        (forward, adjoint, small),
-        [(3, 6, (x, 1, 1), ((0, 2 + x), (1, 2 * x + 1))) for x in range(2)]
-        + [(3, 6, (x, 0, 1), ((3, x), (1, 2 * x))) for x in range(2)]
-        + [(3, 3, (x, 1, 0), ((0, x), None)) for x in range(2)]
-        + [(0, 3, (1, a, b), ((2, 2 * a + b),)) for a, b in bits],
-        (4, 4, 4, 2),
-    )
-    shear_1 = swap(shear_1, "b")
-    lame_1 = swap(lame_1, "a")
-    density_1 = swap(density_1, "x")
-    later = lax.optimization_barrier((small, lame_high))[0]
-    lame_low, shear_low, shear_high, density_low, density_high = gradient(
+    args = (forward, adjoint, small)
+    v = gradient(
+        args,
+        [
+            (3, 6, (1, 1, 1), (("lame11", 1), ("shear11", 1))),
+            (3, 6, (0, 1, 1), (("lame11", 0), ("shear10_1", 0))),
+            (3, 6, (1, 0, 1), (("lame01_1", 0), ("shear11", 0))),
+            (0, 3, (1, 1, 0), (("density11", 0),)),
+            (0, 3, (1, 1, 1), (("density11", 1),)),
+        ],
+        [],
+        {"lame11": 2, "shear11": 2, "density11": 2, "shear10_1": 1, "lame01_1": 1},
+    )
+    shear11 = swap(v["shear11"], "b")
+    lame11 = swap(v["lame11"], "a")
+    density11 = swap(v["density11"], "x")
+    v |= gradient(
+        args,
+        [
+            (3, 6, (0, 0, 1), (("lame01_0", 0), ("shear10", 0))),
+            (3, 6, (0, 1, 0), (("lame10", 0), ("shear00_1", 0))),
+            (3, 6, (1, 1, 0), (("lame10", 1), ("shear01_1", 0))),
+            (0, 3, (1, 0, 0), (("density10", 0),)),
+            (0, 3, (1, 0, 1), (("density10", 1),)),
+        ],
+        [(v["shear10_1"], ("shear10", 1))],
+        {
+            "lame10": 2, "shear10": 2, "density10": 2,
+            "lame01_0": 1, "shear00_1": 1, "shear01_1": 1,
+        },
+    )
+    shear10 = swap(v["shear10"], "b")
+    lame10 = swap(v["lame10"], "a")
+    density10 = swap(v["density10"], "x")
+    later = lax.optimization_barrier((small, v["lame10"]))[0]
+    v |= gradient(
         (forward, adjoint, later),
-        [(3, 6, (x, 0, 0), ((0, x), (1 + x, 0))) for x in range(2)]
-        + [(3, 6, (x, 1, 0), (None, (1 + x, 1))) for x in range(2)]
-        + [(0, 3, (0, a, b), ((3 + a, b),)) for a, b in bits],
-        (2, 2, 2, 2, 2),
-    )
-
-    def finish(first, low, high, dims):
-        second = swap(high + first[2:4], dims[0])
-        third = swap(low[1] + first[1] + second[1], dims[1])
-        return low[0] + first[0] + second[0] + third
-
-    shear = finish(shear_1, shear_low, shear_high, "xa")
-    lame = finish(lame_1, lame_low, lame_high, "bx")
-    density = finish(density_1, density_low, density_high, "ab")
+        [
+            (3, 6, (1, 0, 0), (("lame00_1", 0), ("shear01_0", 0))),
+            (0, 3, (0, 1, 0), (("density01_0", 0),)),
+            (0, 3, (0, 1, 1), (("density01_1", 0),)),
+            (3, 6, (0, 0, 0), (("lame00_0", 0), ("shear00_0", 0))),
+            (0, 3, (0, 0, 0), (("density00_0", 0),)),
+            (0, 3, (0, 0, 1), (("density00_1", 0),)),
+        ],
+        [],
+        {
+            "lame00_0": 1, "lame00_1": 1, "shear00_0": 1, "shear01_0": 1,
+            "density00_0": 1, "density00_1": 1, "density01_0": 1, "density01_1": 1,
+        },
+    )
+
+    def finish(name, in11, in10, dims):
+        def mine(bits):
+            return v[name + bits][0]
+
+        in01_1 = swap(mine("01_1") + in11[1], dims[0])
+        in01_0 = swap(mine("01_0") + in11[0], dims[0])
+        sent, rest = add_up(v[name + "00_1"], v[name + "00_0"], in10, in01_1)
+        return rest + in01_0 + swap(sent, dims[1])
+
+    shear = finish("shear", shear11, shear10, "xa")
+    lame = finish("lame", lame11, lame10, "bx")
+    density = finish("density", density11, density10, "ab")
     cells = jnp.concatenate([lame, shear, density], axis=0)
     along_x = smooth(cells, "gx", spread_x * RADIUS, False)
     smoothed = smooth(along_x, "gy", spread_y * RADIUS, True)

time: 54.5 us -> 53.5 us (0.982)
  waiting for transfers between devices: 15.9 us -> 12.2 us
  starting transfers between devices: 25.2 us -> 28.1 us
    ppermute x9 -> x15, waiting for transfers between devices: 11.8 us -> 7.62 us  [swap(): return lax.ppermute(v, 'shot', [(i, i ^ flips[dim]) for i in range(shots)])]
    ppermute x2, starting transfers between devices: 10.8 us -> 12.6 us  [smooth(): second = lax.ppermute(jnp.where(even, head, tail), axis, swaps[1])]
    ppermute x9 -> x15, starting transfers between devices: 14.5 us -> 15.5 us  [swap(): return lax.ppermute(v, 'shot', [(i, i ^ flips[dim]) for i in range(shots)])]
    pallas_call x6 -> x10, Pallas kernels: 11.4 us -> 11.3 us  [the longest x3 9.15 us: gradient(): pl.pallas_call(functools.partial(gradient_kernel, steps, len(names), kept...]
  transfers between devices with their start and end apart: 13 -> 19, of which waited for: 8 -> 9; matrix products, arithmetic and copies ran while one was open for 0% -> 0% of each run, Pallas kernels for 9% -> 13%
where the time goes in v2:
time: 53.5 us; the launch traced here: 53.4 us
  starting transfers between devices  28.1 us (53%)
  waiting for transfers between devices  12.2 us (23%)
  Pallas kernels  11.3 us (21%)
  other arithmetic  0.99 us (2%)
  between operations  0.82 us (2%)
    ppermute x15, starting transfers between devices, swap(): return lax.ppermute(v, 'shot', [(i, i ^ flips[dim]) for i in range(shots)])  15.5 us
    ppermute x2, starting transfers between devices, smooth(): second = lax.ppermute(jnp.where(even, head, tail), axis, swaps[1])  12.6 us
    pallas_call x3, Pallas kernels, gradient(): pl.pallas_call(functools.partial(gradient_kernel, steps, len(names), kept...  9.15 us
    ppermute x15, waiting for transfers between devices, swap(): return lax.ppermute(v, 'shot', [(i, i ^ flips[dim]) for i in range(shots)])  7.62 us
    ppermute x2, waiting for transfers between devices, smooth(): second = lax.ppermute(jnp.where(even, head, tail), axis, swaps[1])  3.1 us
    ppermute x2, waiting for transfers between devices, smooth(): first = lax.ppermute(jnp.where(even, tail, head), axis, swaps[0])  1.46 us
    pallas_call x2, Pallas kernels, smooth(): pl.pallas_call(outer_kernel, out_shape=(jax.ShapeDtypeStruct if last else...  1.22 us
  transfers between devices with their start and end apart: 19, of which 9 were waited for; matrix products, arithmetic and copies ran while one was open for 0% of the time, Pallas kernels for 13%

profile of v2, /device:TPU:1, one launch (start us, length us, event | category | flops | bytes accessed | tf_op | source)
XLA Modules:
  0.0 53.4 jit_solution(5608389693892124474)
XLA Ops:
  0.7 0.7 %pad_add_fusion.refs_2_ = s32[1,1,5]{2,1,0:T(1,128)S(1)} fusion(s32[1,1,1]{2,1,0:T(1,128)S(6)} %copy.6, s32[1,1,2]{2,1,0:T(1,128)} %bitcast.15, s32[1,1,2]{2,1,0:T(1,128)} %bitcast.16), kind=kLoop, calls=%fused_computation.20 | loop fusion | flops 10 | bytes 40 | tf_op jit(solution)/shard_map/concatenate | solution.py:220
  1.4 3.0 %shard_map.55 = (f32[2,2,128,128]{3,2,1,0:T(8,128)S(1)}, f32[2,2,128,128]{3,2,1,0:T(8,128)S(1)}, f32[2,2,128,128]{3,2,1,0:T(8,128)S(1)}, f32[1,2,128,128]{3,2,1,0:T(8,128)S(1)}, f32[1,2,128,128]{3,2,1,0:T(8,128)S(1)}) custom-call(bf16[1,2,9,16,128,128]{5,4,3,2,1,0:T(8,128)(2,1)} %refs_0_.5, bf16[1,2,9,16,128,128]{5,4,3,2,1,0:T(8,128)(2,1)} %refs_1_.5, ...), custom_call_target="tpu_custom_call" | custom-call | tf_op jit(solution)/shard_map/pallas_call | solution.py:101
  4.5 2.5 %collective-permute-start.1 = (f32[2,2,128,128]{3,2,1,0:T(8,128)S(1)}, f32[2,2,128,128]{3,2,1,0:T(8,128)S(1)}, u32[]{:S(2)}, u32[]{:S(2)}) collective-permute-start(f32[2,2,128,128]{3,2,1,0:T(8,128)S(1)} %get-tuple-element.41), channel_id=1, source_target_pairs={{0,16},{16,0},{32,48},{48,32},{64,80},{80,64},{96,112},{112,96},{1... | collective-permute-start | bytes 786440 | tf_op jit(solution)/shard_map/ppermute | solution.py:225
  7.0 1.2 %collective-permute-start.11 = (f32[2,2,128,128]{3,2,1,0:T(8,128)S(1)}, f32[2,2,128,128]{3,2,1,0:T(8,128)S(1)}, u32[]{:S(2)}, u32[]{:S(2)}) collective-permute-start(f32[2,2,128,128]{3,2,1,0:T(8,128)S(1)} %get-tuple-element.57), channel_id=1, source_target_pairs={{0,64},{16,80},{32,96},{48,112},{64,0},{80,16},{96,32},{112,48},{1... | collective-permute-start | bytes 786440 | tf_op jit(solution)/shard_map/ppermute | solution.py:225
  8.2 2.2 %collective-permute-start.6 = (f32[2,2,128,128]{3,2,1,0:T(8,128)S(1)}, f32[2,2,128,128]{3,2,1,0:T(8,128)S(1)}, u32[]{:S(2)}, u32[]{:S(2)}) collective-permute-start(f32[2,2,128,128]{3,2,1,0:T(8,128)S(1)} %get-tuple-element.49), channel_id=1, source_target_pairs={{0,48},{16,32},{32,16},{48,0},{64,112},{80,96},{96,80},{112,64},{1... | collective-permute-start | bytes 786440 | tf_op jit(solution)/shard_map/ppermute | solution.py:225
  10.4 3.0 %shard_map.56 = (f32[2,2,128,128]{3,2,1,0:T(8,128)S(1)}, f32[2,2,128,128]{3,2,1,0:T(8,128)S(1)}, f32[2,2,128,128]{3,2,1,0:T(8,128)S(1)}, f32[1,2,128,128]{3,2,1,...) custom-call(bf16[1,2,9,16,128,128]{5,4,3,2,1,0:T(8,128)(2,1)} %refs_0_.5, ...), custom_call_target="tpu_custom_call" | custom-call | tf_op jit(solution)/shard_map/pallas_call | solution.py:101
  13.5 0.5 collective-permute-start.5
  14.0 0.4 collective-permute-start
  14.4 3.1 %shard_map.57 = (f32[1,2,128,128]{3,2,1,0:T(8,128)S(1)}, f32[1,2,128,128]{3,2,1,0:T(8,128)S(1)}, f32[1,2,128,128]{3,2,1,0:T(8,128)S(1)}, f32[1,2,128,128]{3,2,1,...) custom-call(bf16[1,2,9,16,128,128]{5,4,3,2,1,0:T(8,128)(2,1)} %refs_, ...), custom_call_target="tpu_custom_call" | custom-call | tf_op jit(solution)/shard_map/pallas_call | solution.py:101
  17.5 0.0 collective-permute-done.1
  17.5 0.3 collective-permute-start.10
  17.9 0.0 collective-permute-done.11
  17.9 2.1 %collective-permute-start.2 = (f32[2,128,128]{2,1,0:T(8,128)S(1)}, f32[2,128,128]{2,1,0:T(8,128)S(1)}, u32[]{:S(2)}, u32[]{:S(2)}) collective-permute-start(f32[2,128,128]{2,1,0:T(8,128)S(1)} %get-tuple-element.70), channel_id=1, source_target_pairs={{0,48},{16,32},{32,16},{48,0},{64,112},{80,96},{96,80},{112,64},{1... | collective-permute-start | bytes 393224 | tf_op jit(solution)/shard_map/ppermute | solution.py:225
  20.0 0.0 collective-permute-done.6
  20.0 0.8 %collective-permute-start.12 = (f32[2,128,128]{2,1,0:T(8,128)S(1)}, f32[2,128,128]{2,1,0:T(8,128)S(1)}, u32[]{:S(2)}, u32[]{:S(2)}) collective-permute-start(f32[2,128,128]{2,1,0:T(8,128)S(1)} %get-tuple-element.74), channel_id=1, source_target_pairs={{0,16},{16,0},{32,48},{48,32},{64,80},{80,64},{96,112},{112,96},{1... | collective-permute-start | bytes 393224 | tf_op jit(solution)/shard_map/ppermute | solution.py:225
  20.8 2.8 %collective-permute-done.10.in10 = f32[2,2,128,128]{3,2,1,0:T(8,128)S(1)} collective-permute-done((f32[2,2,128,128]{3,2,1,0:T(8,128)S(1)}, f32[2,2,128,128]{3,2,1,0:T(8,128)S(1)}, u32[]{:S(2)}, u32[]{:S(2)}) %collective-permute-start.10) | collective-permute-done | bytes 262176 | tf_op jit(solution)/shard_map/ppermute | solution.py:225
  23.6 0.3 collective-permute-start.7
  23.9 0.3 collective-permute-done.12.in01_1
  24.2 0.7 %collective-permute-start.13 = (f32[2,128,128]{2,1,0:T(8,128)S(1)}, f32[2,128,128]{2,1,0:T(8,128)S(1)}, u32[]{:S(2)}, u32[]{:S(2)}) collective-permute-start(f32[2,128,128]{2,1,0:T(8,128)S(1)} %get-tuple-element.73), channel_id=1, source_target_pairs={{0,16},{16,0},{32,48},{48,32},{64,80},{80,64},{96,112},{112,96},{1... | collective-permute-start | bytes 393224 | tf_op jit(solution)/shard_map/ppermute | solution.py:225
  24.9 0.0 collective-permute-done.in10
  25.0 2.1 %collective-permute-start.14 = (f32[2,128,128]{2,1,0:T(8,128)S(1)}, f32[2,128,128]{2,1,0:T(8,128)S(1)}, u32[]{:S(2)}, u32[]{:S(2)}) collective-permute-start(f32[2,128,128]{2,1,0:T(8,128)S(1)} %get-tuple-element.60), channel_id=1, source_target_pairs={{0,48},{16,32},{32,16},{48,0},{64,112},{80,96},{96,80},{112,64},{1... | collective-permute-start | bytes 393224 | tf_op jit(solution)/shard_map/ppermute | solution.py:225
  27.1 0.0 collective-permute-done.2.in01_1
  27.1 0.7 %collective-permute-start.3 = (f32[2,128,128]{2,1,0:T(8,128)S(1)}, f32[2,128,128]{2,1,0:T(8,128)S(1)}, u32[]{:S(2)}, u32[]{:S(2)}) collective-permute-start(f32[2,128,128]{2,1,0:T(8,128)S(1)} %get-tuple-element.69), channel_id=1, source_target_pairs={{0,48},{16,32},{32,16},{48,0},{64,112},{80,96},{96,80},{112,64},{1... | collective-permute-start | bytes 393224 | tf_op jit(solution)/shard_map/ppermute | solution.py:225
  27.8 0.0 collective-permute-done.5.in10
  27.8 1.3 %collective-permute-start.8 = (f32[2,128,128]{2,1,0:T(8,128)S(1)}, f32[2,128,128]{2,1,0:T(8,128)S(1)}, u32[]{:S(2)}, u32[]{:S(2)}) collective-permute-start(f32[2,128,128]{2,1,0:T(8,128)S(1)} %get-tuple-element.71), channel_id=1, source_target_pairs={{0,64},{16,80},{32,96},{48,112},{64,0},{80,16},{96,32},{112,48},{1... | collective-permute-start | bytes 393224 | tf_op jit(solution)/shard_map/ppermute | solution.py:225
  29.1 0.0 collective-permute-done.7.in01_1
  29.1 0.3 collective-permute-start.4
  29.3 0.0 collective-permute-done.13
  29.4 0.1 collective-permute-start.9
  29.5 0.6 %collective-permute-done.14 = f32[2,128,128]{2,1,0:T(8,128)S(1)} collective-permute-done((f32[2,128,128]{2,1,0:T(8,128)S(1)}, f32[2,128,128]{2,1,0:T(8,128)S(1)}, u32[]{:S(2)}, u32[]{:S(2)}) %collective-permute-start.14) | collective-permute-done | bytes 131104 | tf_op jit(solution)/shard_map/ppermute | solution.py:225
  30.1 2.0 %collective-permute-done.3 = f32[2,128,128]{2,1,0:T(8,128)S(1)} collective-permute-done((f32[2,128,128]{2,1,0:T(8,128)S(1)}, f32[2,128,128]{2,1,0:T(8,128)S(1)}, u32[]{:S(2)}, u32[]{:S(2)}) %collective-permute-start.3) | collective-permute-done | bytes 131104 | tf_op jit(solution)/shard_map/ppermute | solution.py:225
  32.1 1.6 %collective-permute-done.4 = f32[2,128,128]{2,1,0:T(8,128)S(1)} collective-permute-done((f32[2,128,128]{2,1,0:T(8,128)S(1)}, f32[2,128,128]{2,1,0:T(8,128)S(1)}, u32[]{:S(2)}, u32[]{:S(2)}) %collective-permute-start.4) | collective-permute-done | bytes 131104 | tf_op jit(solution)/shard_map/ppermute | solution.py:225
  33.7 0.0 collective-permute-done.8
  33.7 0.3 collective-permute-done.9
  34.1 2.8 %collective-permute-start.16 = (f32[6,16,128]{2,1,0:T(8,128)S(1)}, f32[6,16,128]{2,1,0:T(8,128)S(1)}, u32[]{:S(2)}, u32[]{:S(2)}) collective-permute-start(f32[6,16,128]{2,1,0:T(8,128)S(1)} %get-tuple-element.67), channel_id=1, source_target_pairs={{0,12},{4,8},{8,4},{12,0},{1,13},{5,9},{9,5},{13,1},{2,14},{6,10},... | collective-permute-start | bytes 147464 | tf_op jit(solution)/shard_map/ppermute | solution.py:179
  36.9 0.0 collective-permute-start.15
  36.9 0.4 shard_map.58
  37.3 1.1 %collective-permute-done.16.odd_in = f32[6,16,128]{2,1,0:T(8,128)S(1)} collective-permute-done((f32[6,16,128]{2,1,0:T(8,128)S(1)}, f32[6,16,128]{2,1,0:T(8,128)S(1)}, u32[]{:S(2)}, u32[]{:S(2)}) %collective-permute-start.16) | collective-permute-done | bytes 49184 | tf_op jit(solution)/shard_map/ppermute | solution.py:179
  38.4 1.5 %collective-permute-done.15.even_in = f32[6,16,128]{2,1,0:T(8,128)S(1)} collective-permute-done((f32[6,16,128]{2,1,0:T(8,128)S(1)}, f32[6,16,128]{2,1,0:T(8,128)S(1)}, u32[]{:S(2)}, u32[]{:S(2)}) %collective-permute-start.15) | collective-permute-done | bytes 49184 | tf_op jit(solution)/shard_map/ppermute | solution.py:178
  39.9 0.2 shard_map.59.cells
  40.1 9.8 %collective-permute-start.18 = (f32[6,16,128]{2,1,0:T(8,128)S(1)}, f32[6,16,128]{2,1,0:T(8,128)S(1)}, u32[]{:S(2)}, u32[]{:S(2)}) collective-permute-start(f32[6,16,128]{2,1,0:T(8,128)S(1)} %get-tuple-element.65), channel_id=1, source_target_pairs={{0,3},{1,2},{2,1},{3,0},{4,7},{5,6},{6,5},{7,4},{8,11},{9,10},{10,... | collective-permute-start | bytes 147464 | tf_op jit(solution)/shard_map/ppermute | solution.py:179
  49.9 0.0 collective-permute-start.17
  49.9 0.4 shard_map.60
  50.3 2.0 %collective-permute-done.18.odd_in = f32[6,16,128]{2,1,0:T(8,128)S(1)} collective-permute-done((f32[6,16,128]{2,1,0:T(8,128)S(1)}, f32[6,16,128]{2,1,0:T(8,128)S(1)}, u32[]{:S(2)}, u32[]{:S(2)}) %collective-permute-start.18) | collective-permute-done | bytes 49184 | tf_op jit(solution)/shard_map/ppermute | solution.py:179
  52.4 0.0 collective-permute-done.17.even_in
  52.4 1.0 %shard_map.61 = f32[6,128,128]{2,1,0:T(8,128)} custom-call(f32[6,128,128]{2,1,0:T(8,128)S(1)} %get-tuple-element.63.inner, bf16[96,128]{1,0:T(8,128)(2,1)S(1)} %get-tuple-element.64.weights, f32[6,16,128]{2,1,0:T(8,128)S(1)} %collective-permute-done.17.even_in, f32[6,16,128]{2,1,0:T(8,128)S(1)} %collective-permute-done.18.odd_in), custom_call_target="tpu_custom_call" | custom-call | tf_op jit(solution)/shard_map/pallas_call | solution.py:191
  (12 shorter events, 0.3 us)
Async XLA Ops:
  4.5 13.0 %collective-permute-start.1 = (f32[2,2,128,128]{3,2,1,0:T(8,128)S(1)}, f32[2,2,128,128]{3,2,1,0:T(8,128)S(1)}, u32[]{:S(2)}, u32[]{:S(2)}) collective-permute-start(f32[2,2,128,128]{3,2,1,0:T(8,128)S(1)} %get-tuple-element.41), channel_id=1, source_target_pairs={{0,16},{16,0},{32,48},{48,32},{64,80},{80,64},{96,112},{112,96},{1... | collective-permute-start | bytes 786440 | tf_op jit(solution)/shard_map/ppermute | solution.py:225
  7.0 10.9 %collective-permute-start.11 = (f32[2,2,128,128]{3,2,1,0:T(8,128)S(1)}, f32[2,2,128,128]{3,2,1,0:T(8,128)S(1)}, u32[]{:S(2)}, u32[]{:S(2)}) collective-permute-start(f32[2,2,128,128]{3,2,1,0:T(8,128)S(1)} %get-tuple-element.57), channel_id=1, source_target_pairs={{0,64},{16,80},{32,96},{48,112},{64,0},{80,16},{96,32},{112,48},{1... | collective-permute-start | bytes 786440 | tf_op jit(solution)/shard_map/ppermute | solution.py:225
  8.2 11.8 %collective-permute-start.6 = (f32[2,2,128,128]{3,2,1,0:T(8,128)S(1)}, f32[2,2,128,128]{3,2,1,0:T(8,128)S(1)}, u32[]{:S(2)}, u32[]{:S(2)}) collective-permute-start(f32[2,2,128,128]{3,2,1,0:T(8,128)S(1)} %get-tuple-element.49), channel_id=1, source_target_pairs={{0,48},{16,32},{32,16},{48,0},{64,112},{80,96},{96,80},{112,64},{1... | collective-permute-start | bytes 786440 | tf_op jit(solution)/shard_map/ppermute | solution.py:225
  13.5 14.3 %collective-permute-start.5 = (f32[2,2,128,128]{3,2,1,0:T(8,128)S(1)}, f32[2,2,128,128]{3,2,1,0:T(8,128)S(1)}, u32[]{:S(2)}, u32[]{:S(2)}) collective-permute-start(f32[2,2,128,128]{3,2,1,0:T(8,128)S(1)} %get-tuple-element.47), channel_id=1, source_target_pairs={{0,48},{16,32},{32,16},{48,0},{64,112},{80,96},{96,80},{112,64},{1... | collective-permute-start | bytes 786440 | tf_op jit(solution)/shard_map/ppermute | solution.py:225
  14.0 10.9 %collective-permute-start = (f32[2,2,128,128]{3,2,1,0:T(8,128)S(1)}, f32[2,2,128,128]{3,2,1,0:T(8,128)S(1)}, u32[]{:S(2)}, u32[]{:S(2)}) collective-permute-start(f32[2,2,128,128]{3,2,1,0:T(8,128)S(1)} %get-tuple-element.36), channel_id=1, source_target_pairs={{0,16},{16,0},{32,48},{48,32},{64,80},{80,64},{96,112},{112,96},{1... | collective-permute-start | bytes 786440 | tf_op jit(solution)/shard_map/ppermute | solution.py:225
  17.5 6.1 %collective-permute-start.10 = (f32[2,2,128,128]{3,2,1,0:T(8,128)S(1)}, f32[2,2,128,128]{3,2,1,0:T(8,128)S(1)}, u32[]{:S(2)}, u32[]{:S(2)}) collective-permute-start(f32[2,2,128,128]{3,2,1,0:T(8,128)S(1)} %get-tuple-element.55), channel_id=1, source_target_pairs={{0,64},{16,80},{32,96},{48,112},{64,0},{80,16},{96,32},{112,48},{1... | collective-permute-start | bytes 786440 | tf_op jit(solution)/shard_map/ppermute | solution.py:225
  17.9 9.2 %collective-permute-start.2 = (f32[2,128,128]{2,1,0:T(8,128)S(1)}, f32[2,128,128]{2,1,0:T(8,128)S(1)}, u32[]{:S(2)}, u32[]{:S(2)}) collective-permute-start(f32[2,128,128]{2,1,0:T(8,128)S(1)} %get-tuple-element.70), channel_id=1, source_target_pairs={{0,48},{16,32},{32,16},{48,0},{64,112},{80,96},{96,80},{112,64},{1... | collective-permute-start | bytes 393224 | tf_op jit(solution)/shard_map/ppermute | solution.py:225
  20.0 4.2 %collective-permute-start.12 = (f32[2,128,128]{2,1,0:T(8,128)S(1)}, f32[2,128,128]{2,1,0:T(8,128)S(1)}, u32[]{:S(2)}, u32[]{:S(2)}) collective-permute-start(f32[2,128,128]{2,1,0:T(8,128)S(1)} %get-tuple-element.74), channel_id=1, source_target_pairs={{0,16},{16,0},{32,48},{48,32},{64,80},{80,64},{96,112},{112,96},{1... | collective-permute-start | bytes 393224 | tf_op jit(solution)/shard_map/ppermute | solution.py:225
  23.6 5.4 %collective-permute-start.7 = (f32[2,128,128]{2,1,0:T(8,128)S(1)}, f32[2,128,128]{2,1,0:T(8,128)S(1)}, u32[]{:S(2)}, u32[]{:S(2)}) collective-permute-start(f32[2,128,128]{2,1,0:T(8,128)S(1)} %get-tuple-element.72), channel_id=1, source_target_pairs={{0,64},{16,80},{32,96},{48,112},{64,0},{80,16},{96,32},{112,48},{1... | collective-permute-start | bytes 393224 | tf_op jit(solution)/shard_map/ppermute | solution.py:225
  24.2 5.2 %collective-permute-start.13 = (f32[2,128,128]{2,1,0:T(8,128)S(1)}, f32[2,128,128]{2,1,0:T(8,128)S(1)}, u32[]{:S(2)}, u32[]{:S(2)}) collective-permute-start(f32[2,128,128]{2,1,0:T(8,128)S(1)} %get-tuple-element.73), channel_id=1, source_target_pairs={{0,16},{16,0},{32,48},{48,32},{64,80},{80,64},{96,112},{112,96},{1... | collective-permute-start | bytes 393224 | tf_op jit(solution)/shard_map/ppermute | solution.py:225
  25.0 5.1 %collective-permute-start.14 = (f32[2,128,128]{2,1,0:T(8,128)S(1)}, f32[2,128,128]{2,1,0:T(8,128)S(1)}, u32[]{:S(2)}, u32[]{:S(2)}) collective-permute-start(f32[2,128,128]{2,1,0:T(8,128)S(1)} %get-tuple-element.60), channel_id=1, source_target_pairs={{0,48},{16,32},{32,16},{48,0},{64,112},{80,96},{96,80},{112,64},{1... | collective-permute-start | bytes 393224 | tf_op jit(solution)/shard_map/ppermute | solution.py:225
  27.1 5.0 %collective-permute-start.3 = (f32[2,128,128]{2,1,0:T(8,128)S(1)}, f32[2,128,128]{2,1,0:T(8,128)S(1)}, u32[]{:S(2)}, u32[]{:S(2)}) collective-permute-start(f32[2,128,128]{2,1,0:T(8,128)S(1)} %get-tuple-element.69), channel_id=1, source_target_pairs={{0,48},{16,32},{32,16},{48,0},{64,112},{80,96},{96,80},{112,64},{1... | collective-permute-start | bytes 393224 | tf_op jit(solution)/shard_map/ppermute | solution.py:225
  27.8 5.9 %collective-permute-start.8 = (f32[2,128,128]{2,1,0:T(8,128)S(1)}, f32[2,128,128]{2,1,0:T(8,128)S(1)}, u32[]{:S(2)}, u32[]{:S(2)}) collective-permute-start(f32[2,128,128]{2,1,0:T(8,128)S(1)} %get-tuple-element.71), channel_id=1, source_target_pairs={{0,64},{16,80},{32,96},{48,112},{64,0},{80,16},{96,32},{112,48},{1... | collective-permute-start | bytes 393224 | tf_op jit(solution)/shard_map/ppermute | solution.py:225
  29.1 4.6 %collective-permute-start.4 = (f32[2,128,128]{2,1,0:T(8,128)S(1)}, f32[2,128,128]{2,1,0:T(8,128)S(1)}, u32[]{:S(2)}, u32[]{:S(2)}) collective-permute-start(f32[2,128,128]{2,1,0:T(8,128)S(1)} %get-tuple-element.44), channel_id=1, source_target_pairs={{0,64},{16,80},{32,96},{48,112},{64,0},{80,16},{96,32},{112,48},{1... | collective-permute-start | bytes 393224 | tf_op jit(solution)/shard_map/ppermute | solution.py:225
  29.4 4.7 %collective-permute-start.9 = (f32[2,128,128]{2,1,0:T(8,128)S(1)}, f32[2,128,128]{2,1,0:T(8,128)S(1)}, u32[]{:S(2)}, u32[]{:S(2)}) collective-permute-start(f32[2,128,128]{2,1,0:T(8,128)S(1)} %get-tuple-element.52), channel_id=1, source_target_pairs={{0,16},{16,0},{32,48},{48,32},{64,80},{80,64},{96,112},{112,96},{1... | collective-permute-start | bytes 393224 | tf_op jit(solution)/shard_map/ppermute | solution.py:225
  34.1 4.3 %collective-permute-start.16 = (f32[6,16,128]{2,1,0:T(8,128)S(1)}, f32[6,16,128]{2,1,0:T(8,128)S(1)}, u32[]{:S(2)}, u32[]{:S(2)}) collective-permute-start(f32[6,16,128]{2,1,0:T(8,128)S(1)} %get-tuple-element.67), channel_id=1, source_target_pairs={{0,12},{4,8},{8,4},{12,0},{1,13},{5,9},{9,5},{13,1},{2,14},{6,10},... | collective-permute-start | bytes 147464 | tf_op jit(solution)/shard_map/ppermute | solution.py:179
  36.9 2.9 %collective-permute-start.15 = (f32[6,16,128]{2,1,0:T(8,128)S(1)}, f32[6,16,128]{2,1,0:T(8,128)S(1)}, u32[]{:S(2)}, u32[]{:S(2)}) collective-permute-start(f32[6,16,128]{2,1,0:T(8,128)S(1)} %get-tuple-element.68), channel_id=1, source_target_pairs={{0,4},{4,0},{8,12},{12,8},{1,5},{5,1},{9,13},{13,9},{2,6},{6,2},{1... | collective-permute-start | bytes 147464 | tf_op jit(solution)/shard_map/ppermute | solution.py:178
  40.1 12.2 %collective-permute-start.18 = (f32[6,16,128]{2,1,0:T(8,128)S(1)}, f32[6,16,128]{2,1,0:T(8,128)S(1)}, u32[]{:S(2)}, u32[]{:S(2)}) collective-permute-start(f32[6,16,128]{2,1,0:T(8,128)S(1)} %get-tuple-element.65), channel_id=1, source_target_pairs={{0,3},{1,2},{2,1},{3,0},{4,7},{5,6},{6,5},{7,4},{8,11},{9,10},{10,... | collective-permute-start | bytes 147464 | tf_op jit(solution)/shard_map/ppermute | solution.py:179
  49.9 2.4 %collective-permute-start.17 = (f32[6,16,128]{2,1,0:T(8,128)S(1)}, f32[6,16,128]{2,1,0:T(8,128)S(1)}, u32[]{:S(2)}, u32[]{:S(2)}) collective-permute-start(f32[6,16,128]{2,1,0:T(8,128)S(1)} %get-tuple-element.66), channel_id=1, source_target_pairs={{0,1},{1,0},{2,3},{3,2},{4,5},{5,4},{6,7},{7,6},{8,9},{9,8},{10,11... | collective-permute-start | bytes 147464 | tf_op jit(solution)/shard_map/ppermute | solution.py:178

commit v3 on v2

--- a/solution.py
+++ b/solution.py
@@ -17,49 +17,71 @@
 spread_y = 0.375
 
 
-def gradient_kernel(steps, n_out, carried, *refs):
-    fwd, adj, small = refs[:3]
-    whole = refs[3 : 3 + len(carried)]
-    outs = refs[3 + len(carried) :][:n_out]
-    taper, sems, *bufs = refs[3 + len(carried) + n_out :]
+def gradient_kernel(steps, n_out, resident, first, *refs):
+    fwd, adj = refs[:2]
+    if first:
+        times, sources, aperture, *refs = refs[2:]
+        outs, refs = refs[:n_out], refs[n_out:]
+        taper, factors, sems, time_cells, source_cells, small_sems, *bufs = refs
+    else:
+        taper, factors, *refs = refs[2:]
+        outs, refs = refs[:n_out], refs[n_out:]
+        sems, *bufs = refs
+    streamed = [i for i in range(2) if not resident[i]]
     shot = lax.axis_index("shot")
     half, z = lax.div(shot, RZ), lax.rem(shot, RZ)
-    copies = []
+    if first:
+        smalls = [
+            pltpu.make_async_copy(times, time_cells, small_sems.at[0]),
+            pltpu.make_async_copy(sources, source_cells, small_sems.at[1]),
+        ]
+        for cp in smalls:
+            cp.start()
+    copies, levels = [], []
     for n, (c0, cn, (x, a, b), _) in enumerate(steps):
         lev = 2 * ((half ^ x) * RZ + (z ^ (a ^ (3 * b))))
+        levels.append(lev)
         copies.append(
             [
                 pltpu.make_async_copy(
-                    src.at[0, :, pl.ds(c0, cn), pl.ds(lev, 2)], bufs[n].at[i], sems.at[n, i]
+                    (fwd, adj)[i].at[0, :, pl.ds(c0, cn), pl.ds(lev, 2)],
+                    bufs[n].at[slot],
+                    sems.at[n, slot],
                 )
-                for i, src in enumerate((fwd, adj))
+                for slot, i in enumerate(streamed)
             ]
         )
     for pair in copies:
         for cp in pair:
             cp.start()
-    for src, (o, i) in zip(whole, carried):
-        outs[o][i] = src[0]
-    times_etc = small[0]
-    t0, t1 = times_etc[:, 0:1], times_etc[:, 1:2]
-    weights = (-(t0.astype(jnp.float32) / 8.0), -((t1 - t0).astype(jnp.float32) / 8.0))
-    inside = times_etc[:, 4:5].astype(jnp.float32)
     shape = taper.shape
-    xs = lax.broadcasted_iota(jnp.int32, shape, 0) + lax.axis_index("gx") * shape[0]
-    ys = lax.broadcasted_iota(jnp.int32, shape, 1) + lax.axis_index("gy") * shape[1]
-    dx = (xs - times_etc[:, 2:3]).astype(jnp.float32)
-    dy = (ys - times_etc[:, 3:4]).astype(jnp.float32)
-    taper[...] = (1.0 - jnp.exp(-(dx * dx + dy * dy) / (2.0 * MUTE * MUTE))) * inside
+    if first:
+        for cp in smalls:
+            cp.wait()
+        t0, t1 = time_cells[:, 0:1], time_cells[:, 1:2]
+        for k, step in enumerate((t0, t1 - t0)):
+            factors[k] = jnp.broadcast_to(-(step.astype(jnp.float32) / 8.0), factors.shape[1:])
+        inside = aperture[0, 0, 0].astype(jnp.float32)
+        xs = lax.broadcasted_iota(jnp.int32, shape, 0) + lax.axis_index("gx") * shape[0]
+        ys = lax.broadcasted_iota(jnp.int32, shape, 1) + lax.axis_index("gy") * shape[1]
+        dx = (xs - source_cells[:, 0:1]).astype(jnp.float32)
+        dy = (ys - source_cells[:, 1:2]).astype(jnp.float32)
+        taper[...] = (1.0 - jnp.exp(-(dx * dx + dy * dy) / (2.0 * MUTE * MUTE))) * inside
+    weights = [factors[k] for k in range(2)]
     for n, (c0, cn, _, where) in enumerate(steps):
         for cp in copies[n]:
             cp.wait()
-        buf = bufs[n]
-
-        def body(lev, carry, buf=buf, c0=c0, cn=cn, where=where):
+        buf = bufs[n] if streamed else None
+
+        def body(lev, carry, buf=buf, first=levels[n], c0=c0, cn=cn, where=where):
             for r in range(0, shape[0], ROWS):
 
                 def load(i, k, c):
-                    return buf[i, k, c, lev, r : r + ROWS, :].astype(jnp.float32)
+                    if resident[i]:
+                        cells = (fwd, adj)[i][0, k, c0 + c, first + lev, r : r + ROWS, :]
+                    else:
+                        cells = buf[streamed.index(i), k, c, lev, r : r + ROWS, :]
+                    return cells.astype(jnp.float32)
 
                 def product(k, c):
                     return load(0, k, c) * load(1, k, c)
@@ -88,29 +110,40 @@
         lax.fori_loop(0, 2, body, 0)
 
 
-def gradient(args, steps, carried, counts):
+def gradient(args, resident, steps, counts):
     names = list(counts)
 
     def place(where):
         return None if where is None else (names.index(where[0]), where[1])
 
     steps = [(*step[:3], tuple(place(w) for w in step[3])) for step in steps]
-    kept = [place(where) for _, where in carried]
     wx, wy = args[0].shape[4:]
-    hbm, vm = pl.BlockSpec(memory_space=pltpu.HBM), pl.BlockSpec(memory_space=pltpu.VMEM)
-    outs = pl.pallas_call(
-        functools.partial(gradient_kernel, steps, len(names), kept),
-        out_shape=[pltpu.VMEM((c, 2, wx, wy), jnp.float32) for c in counts.values()],
-        in_specs=[hbm, hbm] + [vm] * (1 + len(kept)),
-        out_specs=[vm] * len(names),
-        scratch_shapes=[
-            pltpu.VMEM((wx, wy), jnp.float32),
-            pltpu.SemaphoreType.DMA((len(steps), 2)),
-        ]
-        + [pltpu.VMEM((2, 2, s[1], 2, wx, wy), jnp.bfloat16) for s in steps],
+    vm = pl.BlockSpec(memory_space=pltpu.VMEM)
+    first = len(args) == 5
+    spaces = [pltpu.VMEM if r else pltpu.HBM for r in resident]
+    waves = [pltpu.with_memory_space_constraint(a, m) for a, m in zip(args[:2], spaces)]
+    rest = list(args[2:])
+    specs = [vm, vm]
+    outs = [pltpu.VMEM((c, 2, wx, wy), jnp.float32) for c in counts.values()]
+    small_scratch = []
+    if first:
+        rest[:2] = [pltpu.with_memory_space_constraint(a, pltpu.HBM) for a in rest[:2]]
+        specs = [pl.BlockSpec(memory_space=m) for m in (pltpu.HBM, pltpu.HBM, pltpu.SMEM)]
+        outs += [pltpu.VMEM((wx, wy), jnp.float32), pltpu.VMEM((2, ROWS, wy), jnp.float32)]
+        small_scratch = [pltpu.VMEM(a.shape, jnp.int32) for a in rest[:2]]
+        small_scratch.append(pltpu.SemaphoreType.DMA((2,)))
+    streams = 2 - sum(resident)
+    results = pl.pallas_call(
+        functools.partial(gradient_kernel, steps, len(names), resident, first),
+        out_shape=outs,
+        in_specs=[pl.BlockSpec(memory_space=m) for m in spaces] + specs,
+        out_specs=[vm] * len(outs),
+        scratch_shapes=[pltpu.SemaphoreType.DMA((len(steps), max(streams, 1)))]
+        + small_scratch
+        + [pltpu.VMEM((streams, 2, s[1], 2, wx, wy), jnp.bfloat16) for s in steps if streams],
         compiler_params=pltpu.CompilerParams(vmem_limit_bytes=12 << 20),
-    )(*args, *(src for src, _ in carried))
-    return dict(zip(names, outs))
+    )(*waves, *rest)
+    return dict(zip(names + ["taper", "factors"], results))
 
 
 def band(first, rows, cols, sigma):
@@ -215,41 +248,39 @@
 
 
 def on_device(forward, adjoint, snap_times, sources, aperture):
-    forward = pltpu.with_memory_space_constraint(forward, pltpu.HBM)
-    adjoint = pltpu.with_memory_space_constraint(adjoint, pltpu.HBM)
-    small = jnp.concatenate([snap_times[None], sources[None], aperture], axis=2)
     shots = lax.axis_size("shot")
     flips = {"x": RZ, "a": 1, "b": 3}
 
     def swap(v, dim):
         return lax.ppermute(v, "shot", [(i, i ^ flips[dim]) for i in range(shots)])
 
-    args = (forward, adjoint, small)
+    args = (forward, adjoint, snap_times, sources, aperture)
     v = gradient(
         args,
+        (False, False),
         [
             (3, 6, (1, 1, 1), (("lame11", 1), ("shear11", 1))),
-            (3, 6, (0, 1, 1), (("lame11", 0), ("shear10_1", 0))),
+            (3, 3, (0, 1, 1), (("lame11", 0), None)),
             (3, 6, (1, 0, 1), (("lame01_1", 0), ("shear11", 0))),
             (0, 3, (1, 1, 0), (("density11", 0),)),
             (0, 3, (1, 1, 1), (("density11", 1),)),
         ],
-        [],
-        {"lame11": 2, "shear11": 2, "density11": 2, "shear10_1": 1, "lame01_1": 1},
+        {"lame11": 2, "shear11": 2, "density11": 2, "lame01_1": 1},
     )
     shear11 = swap(v["shear11"], "b")
     lame11 = swap(v["lame11"], "a")
     density11 = swap(v["density11"], "x")
     v |= gradient(
-        args,
+        (forward, adjoint, v["taper"], v["factors"]),
+        (True, True),
         [
             (3, 6, (0, 0, 1), (("lame01_0", 0), ("shear10", 0))),
+            (3, 6, (0, 1, 1), (None, ("shear10", 1))),
             (3, 6, (0, 1, 0), (("lame10", 0), ("shear00_1", 0))),
             (3, 6, (1, 1, 0), (("lame10", 1), ("shear01_1", 0))),
             (0, 3, (1, 0, 0), (("density10", 0),)),
             (0, 3, (1, 0, 1), (("density10", 1),)),
         ],
-        [(v["shear10_1"], ("shear10", 1))],
         {
             "lame10": 2, "shear10": 2, "density10": 2,
             "lame01_0": 1, "shear00_1": 1, "shear01_1": 1,
@@ -258,9 +289,10 @@
     shear10 = swap(v["shear10"], "b")
     lame10 = swap(v["lame10"], "a")
     density10 = swap(v["density10"], "x")
-    later = lax.optimization_barrier((small, v["lame10"]))[0]
+    taper = lax.optimization_barrier((v["taper"], v["lame10"]))[0]
     v |= gradient(
-        (forward, adjoint, later),
+        (forward, adjoint, taper, v["factors"]),
+        (True, True),
         [
             (3, 6, (1, 0, 0), (("lame00_1", 0), ("shear01_0", 0))),
             (0, 3, (0, 1, 0), (("density01_0", 0),)),
@@ -269,7 +301,6 @@
             (0, 3, (0, 0, 0), (("density00_0", 0),)),
             (0, 3, (0, 0, 1), (("density00_1", 0),)),
         ],
-        [],
         {
             "lame00_0": 1, "lame00_1": 1, "shear00_0": 1, "shear01_0": 1,
             "density00_0": 1, "density00_1": 1, "density01_0": 1, "density01_1": 1,

time: 53.5 us -> 52.1 us (0.974)
  Pallas kernels: 11.3 us -> 7.75 us
  starting transfers between devices: 28.1 us -> 30.4 us
  other arithmetic: 0.99 us -> 0.21 us
  waiting for transfers between devices: 12.2 us -> 12.8 us
    ppermute x15, starting transfers between devices: 15.5 us -> 19.1 us  [swap(): return lax.ppermute(v, 'shot', [(i, i ^ flips[dim]) for i in range(shots)])]
    pallas_call x3, Pallas kernels: 9.15 us -> 5.61 us  [gradient(): pl.pallas_call(functools.partial(gradient_kernel, steps, len(names), resi...]
    ppermute x2, starting transfers between devices: 12.6 us -> 11.3 us  [smooth(): second = lax.ppermute(jnp.where(even, head, tail), axis, swaps[1])]
    concatenate x1 -> x0, other arithmetic: 0.75 us -> none  [on_device(): small = jnp.concatenate([snap_times[None], sources[None], aperture], axis=2)]
    ppermute x15, waiting for transfers between devices: 7.62 us -> 8.33 us  [swap(): return lax.ppermute(v, 'shot', [(i, i ^ flips[dim]) for i in range(shots)])]
  transfers between devices with their start and end apart: 19 -> 19, of which waited for: 9 -> 9; matrix products, arithmetic and copies ran while one was open for 0% -> 0% of each run, Pallas kernels for 13% -> 7%
where the time goes in v3:
time: 52.1 us; the launch traced here: 52 us
  starting transfers between devices  30.4 us (58%)
  waiting for transfers between devices  12.8 us (25%)
  Pallas kernels  7.75 us (15%)
  between operations  0.84 us (2%)
    ppermute x15, starting transfers between devices, swap(): return lax.ppermute(v, 'shot', [(i, i ^ flips[dim]) for i in range(shots)])  19.1 us
    ppermute x2, starting transfers between devices, smooth(): second = lax.ppermute(jnp.where(even, head, tail), axis, swaps[1])  11.3 us
    ppermute x15, waiting for transfers between devices, swap(): return lax.ppermute(v, 'shot', [(i, i ^ flips[dim]) for i in range(shots)])  8.33 us
    pallas_call x3, Pallas kernels, gradient(): pl.pallas_call(functools.partial(gradient_kernel, steps, len(names), resi...  5.61 us
    ppermute x2, waiting for transfers between devices, smooth(): second = lax.ppermute(jnp.where(even, head, tail), axis, swaps[1])  3.03 us
    ppermute x2, waiting for transfers between devices, smooth(): first = lax.ppermute(jnp.where(even, tail, head), axis, swaps[0])  1.46 us
    pallas_call x2, Pallas kernels, smooth(): pl.pallas_call(outer_kernel, out_shape=(jax.ShapeDtypeStruct if last else...  1.22 us
  transfers between devices with their start and end apart: 19, of which 9 were waited for; matrix products, arithmetic and copies ran while one was open for 0% of the time, Pallas kernels for 7%

profile of v3, /device:TPU:1, one launch (start us, length us, event | category | flops | bytes accessed | tf_op | source)
XLA Modules:
  0.0 52.0 jit_solution(1229645589618641192)
XLA Ops:
  0.7 0.0 copy-start
  0.7 0.0 copy-start.1
  0.7 3.0 %shard_map.55 = (f32[2,2,128,128]{3,2,1,0:T(8,128)S(1)}, f32[2,2,128,128]{3,2,1,0:T(8,128)S(1)}, f32[2,2,128,128]{3,2,1,0:T(8,128)S(1)}, f32[1,2,128,128]{3,2,1,...) custom-call(bf16[1,2,9,16,128,128]{5,4,3,2,1,0:T(8,128)(2,1)} %refs_0_.5, ...), custom_call_target="tpu_custom_call" | custom-call | tf_op jit(solution)/shard_map/pallas_call | solution.py:136
  3.6 2.5 %collective-permute-start.1 = (f32[2,2,128,128]{3,2,1,0:T(8,128)S(1)}, f32[2,2,128,128]{3,2,1,0:T(8,128)S(1)}, u32[]{:S(2)}, u32[]{:S(2)}) collective-permute-start(f32[2,2,128,128]{3,2,1,0:T(8,128)S(1)} %get-tuple-element.43), channel_id=1, source_target_pairs={{0,16},{16,0},{32,48},{48,32},{64,80},{80,64},{96,112},{112,96},{1... | collective-permute-start | bytes 786440 | tf_op jit(solution)/shard_map/ppermute | solution.py:255
  6.2 1.2 %collective-permute-start.11 = (f32[2,2,128,128]{3,2,1,0:T(8,128)S(1)}, f32[2,2,128,128]{3,2,1,0:T(8,128)S(1)}, u32[]{:S(2)}, u32[]{:S(2)}) collective-permute-start(f32[2,2,128,128]{3,2,1,0:T(8,128)S(1)} %get-tuple-element.59), channel_id=1, source_target_pairs={{0,64},{16,80},{32,96},{48,112},{64,0},{80,16},{96,32},{112,48},{1... | collective-permute-start | bytes 786440 | tf_op jit(solution)/shard_map/ppermute | solution.py:255
  7.4 2.2 %collective-permute-start.6 = (f32[2,2,128,128]{3,2,1,0:T(8,128)S(1)}, f32[2,2,128,128]{3,2,1,0:T(8,128)S(1)}, u32[]{:S(2)}, u32[]{:S(2)}) collective-permute-start(f32[2,2,128,128]{3,2,1,0:T(8,128)S(1)} %get-tuple-element.51), channel_id=1, source_target_pairs={{0,48},{16,32},{32,16},{48,0},{64,112},{80,96},{96,80},{112,64},{1... | collective-permute-start | bytes 786440 | tf_op jit(solution)/shard_map/ppermute | solution.py:255
  9.6 0.0 copy-done.1
  9.6 1.5 %shard_map.56 = (f32[2,2,128,128]{3,2,1,0:T(8,128)S(1)}, f32[2,2,128,128]{3,2,1,0:T(8,128)S(1)}, f32[2,2,128,128]{3,2,1,0:T(8,128)S(1)}, f32[1,2,128,128]{3,2,1,...) custom-call(bf16[1,2,9,16,128,128]{5,4,3,2,1,0:T(8,128)(2,1)S(1)} %copy-done, ...), custom_call_target="tpu_custom_call" | custom-call | tf_op jit(solution)/shard_map/pallas_call | solution.py:136
  11.1 3.7 %collective-permute-start.5 = (f32[2,2,128,128]{3,2,1,0:T(8,128)S(1)}, f32[2,2,128,128]{3,2,1,0:T(8,128)S(1)}, u32[]{:S(2)}, u32[]{:S(2)}) collective-permute-start(f32[2,2,128,128]{3,2,1,0:T(8,128)S(1)} %get-tuple-element.49), channel_id=1, source_target_pairs={{0,48},{16,32},{32,16},{48,0},{64,112},{80,96},{96,80},{112,64},{1... | collective-permute-start | bytes 786440 | tf_op jit(solution)/shard_map/ppermute | solution.py:255
  14.9 0.0 collective-permute-start
  14.9 1.2 %shard_map.57 = (f32[1,2,128,128]{3,2,1,0:T(8,128)S(1)}, f32[1,2,128,128]{3,2,1,0:T(8,128)S(1)}, f32[1,2,128,128]{3,2,1,0:T(8,128)S(1)}, f32[1,2,128,128]{3,2,1,...) custom-call(bf16[1,2,9,16,128,128]{5,4,3,2,1,0:T(8,128)(2,1)S(1)} %c, ...), custom_call_target="tpu_custom_call" | custom-call | tf_op jit(solution)/shard_map/pallas_call | solution.py:136
  16.0 0.0 collective-permute-done.1
  16.0 1.3 %collective-permute-start.10 = (f32[2,2,128,128]{3,2,1,0:T(8,128)S(1)}, f32[2,2,128,128]{3,2,1,0:T(8,128)S(1)}, u32[]{:S(2)}, u32[]{:S(2)}) collective-permute-start(f32[2,2,128,128]{3,2,1,0:T(8,128)S(1)} %get-tuple-element.57), channel_id=1, source_target_pairs={{0,64},{16,80},{32,96},{48,112},{64,0},{80,16},{96,32},{112,48},{1... | collective-permute-start | bytes 786440 | tf_op jit(solution)/shard_map/ppermute | solution.py:255
  17.4 0.0 collective-permute-done.11
  17.4 0.3 collective-permute-start.2
  17.7 0.0 collective-permute-done.6
  17.7 1.3 %collective-permute-start.12 = (f32[2,128,128]{2,1,0:T(8,128)S(1)}, f32[2,128,128]{2,1,0:T(8,128)S(1)}, u32[]{:S(2)}, u32[]{:S(2)}) collective-permute-start(f32[2,128,128]{2,1,0:T(8,128)S(1)} %get-tuple-element.76), channel_id=1, source_target_pairs={{0,16},{16,0},{32,48},{48,32},{64,80},{80,64},{96,112},{112,96},{1... | collective-permute-start | bytes 393224 | tf_op jit(solution)/shard_map/ppermute | solution.py:255
  19.1 3.9 %collective-permute-done.10.in10 = f32[2,2,128,128]{3,2,1,0:T(8,128)S(1)} collective-permute-done((f32[2,2,128,128]{3,2,1,0:T(8,128)S(1)}, f32[2,2,128,128]{3,2,1,0:T(8,128)S(1)}, u32[]{:S(2)}, u32[]{:S(2)}) %collective-permute-start.10) | collective-permute-done | bytes 262176 | tf_op jit(solution)/shard_map/ppermute | solution.py:255
  23.0 1.2 %collective-permute-start.7 = (f32[2,128,128]{2,1,0:T(8,128)S(1)}, f32[2,128,128]{2,1,0:T(8,128)S(1)}, u32[]{:S(2)}, u32[]{:S(2)}) collective-permute-start(f32[2,128,128]{2,1,0:T(8,128)S(1)} %get-tuple-element.74), channel_id=1, source_target_pairs={{0,64},{16,80},{32,96},{48,112},{64,0},{80,16},{96,32},{112,48},{1... | collective-permute-start | bytes 393224 | tf_op jit(solution)/shard_map/ppermute | solution.py:255
  24.2 0.3 collective-permute-done.12.in01_1
  24.6 0.9 %collective-permute-start.13 = (f32[2,128,128]{2,1,0:T(8,128)S(1)}, f32[2,128,128]{2,1,0:T(8,128)S(1)}, u32[]{:S(2)}, u32[]{:S(2)}) collective-permute-start(f32[2,128,128]{2,1,0:T(8,128)S(1)} %get-tuple-element.75), channel_id=1, source_target_pairs={{0,16},{16,0},{32,48},{48,32},{64,80},{80,64},{96,112},{112,96},{1... | collective-permute-start | bytes 393224 | tf_op jit(solution)/shard_map/ppermute | solution.py:255
  25.5 0.0 collective-permute-done.in10
  25.5 0.5 collective-permute-start.14
  25.9 0.0 collective-permute-done.2.in01_1
  25.9 2.3 %collective-permute-start.3 = (f32[2,128,128]{2,1,0:T(8,128)S(1)}, f32[2,128,128]{2,1,0:T(8,128)S(1)}, u32[]{:S(2)}, u32[]{:S(2)}) collective-permute-start(f32[2,128,128]{2,1,0:T(8,128)S(1)} %get-tuple-element.71), channel_id=1, source_target_pairs={{0,48},{16,32},{32,16},{48,0},{64,112},{80,96},{96,80},{112,64},{1... | collective-permute-start | bytes 393224 | tf_op jit(solution)/shard_map/ppermute | solution.py:255
  28.3 0.0 collective-permute-done.5.in10
  28.3 0.7 %collective-permute-start.8 = (f32[2,128,128]{2,1,0:T(8,128)S(1)}, f32[2,128,128]{2,1,0:T(8,128)S(1)}, u32[]{:S(2)}, u32[]{:S(2)}) collective-permute-start(f32[2,128,128]{2,1,0:T(8,128)S(1)} %get-tuple-element.73), channel_id=1, source_target_pairs={{0,64},{16,80},{32,96},{48,112},{64,0},{80,16},{96,32},{112,48},{1... | collective-permute-start | bytes 393224 | tf_op jit(solution)/shard_map/ppermute | solution.py:255
  29.0 0.0 collective-permute-done.7.in01_1
  29.0 0.8 %collective-permute-start.4 = (f32[2,128,128]{2,1,0:T(8,128)S(1)}, f32[2,128,128]{2,1,0:T(8,128)S(1)}, u32[]{:S(2)}, u32[]{:S(2)}) collective-permute-start(f32[2,128,128]{2,1,0:T(8,128)S(1)} %get-tuple-element.46), channel_id=1, source_target_pairs={{0,64},{16,80},{32,96},{48,112},{64,0},{80,16},{96,32},{112,48},{1... | collective-permute-start | bytes 393224 | tf_op jit(solution)/shard_map/ppermute | solution.py:255
  29.9 0.0 collective-permute-done.13
  29.9 0.1 collective-permute-start.9
  30.0 0.6 %collective-permute-done.14 = f32[2,128,128]{2,1,0:T(8,128)S(1)} collective-permute-done((f32[2,128,128]{2,1,0:T(8,128)S(1)}, f32[2,128,128]{2,1,0:T(8,128)S(1)}, u32[]{:S(2)}, u32[]{:S(2)}) %collective-permute-start.14) | collective-permute-done | bytes 131104 | tf_op jit(solution)/shard_map/ppermute | solution.py:255
  30.6 1.4 %collective-permute-done.3 = f32[2,128,128]{2,1,0:T(8,128)S(1)} collective-permute-done((f32[2,128,128]{2,1,0:T(8,128)S(1)}, f32[2,128,128]{2,1,0:T(8,128)S(1)}, u32[]{:S(2)}, u32[]{:S(2)}) %collective-permute-start.3) | collective-permute-done | bytes 131104 | tf_op jit(solution)/shard_map/ppermute | solution.py:255
  32.0 1.9 %collective-permute-done.4 = f32[2,128,128]{2,1,0:T(8,128)S(1)} collective-permute-done((f32[2,128,128]{2,1,0:T(8,128)S(1)}, f32[2,128,128]{2,1,0:T(8,128)S(1)}, u32[]{:S(2)}, u32[]{:S(2)}) %collective-permute-start.4) | collective-permute-done | bytes 131104 | tf_op jit(solution)/shard_map/ppermute | solution.py:255
  33.9 0.0 collective-permute-done.8
  33.9 0.2 collective-permute-done.9
  34.2 2.8 %collective-permute-start.16 = (f32[6,16,128]{2,1,0:T(8,128)S(1)}, f32[6,16,128]{2,1,0:T(8,128)S(1)}, u32[]{:S(2)}, u32[]{:S(2)}) collective-permute-start(f32[6,16,128]{2,1,0:T(8,128)S(1)} %get-tuple-element.69), channel_id=1, source_target_pairs={{0,12},{4,8},{8,4},{12,0},{1,13},{5,9},{9,5},{13,1},{2,14},{6,10},... | collective-permute-start | bytes 147464 | tf_op jit(solution)/shard_map/ppermute | solution.py:212
  37.0 0.0 collective-permute-start.15
  37.0 0.4 shard_map.58
  37.4 1.1 %collective-permute-done.16.odd_in = f32[6,16,128]{2,1,0:T(8,128)S(1)} collective-permute-done((f32[6,16,128]{2,1,0:T(8,128)S(1)}, f32[6,16,128]{2,1,0:T(8,128)S(1)}, u32[]{:S(2)}, u32[]{:S(2)}) %collective-permute-start.16) | collective-permute-done | bytes 49184 | tf_op jit(solution)/shard_map/ppermute | solution.py:212
  38.5 1.5 %collective-permute-done.15.even_in = f32[6,16,128]{2,1,0:T(8,128)S(1)} collective-permute-done((f32[6,16,128]{2,1,0:T(8,128)S(1)}, f32[6,16,128]{2,1,0:T(8,128)S(1)}, u32[]{:S(2)}, u32[]{:S(2)}) %collective-permute-start.15) | collective-permute-done | bytes 49184 | tf_op jit(solution)/shard_map/ppermute | solution.py:211
  39.9 0.2 shard_map.59.cells
  40.2 8.5 %collective-permute-start.18 = (f32[6,16,128]{2,1,0:T(8,128)S(1)}, f32[6,16,128]{2,1,0:T(8,128)S(1)}, u32[]{:S(2)}, u32[]{:S(2)}) collective-permute-start(f32[6,16,128]{2,1,0:T(8,128)S(1)} %get-tuple-element.67), channel_id=1, source_target_pairs={{0,3},{1,2},{2,1},{3,0},{4,7},{5,6},{6,5},{7,4},{8,11},{9,10},{10,... | collective-permute-start | bytes 147464 | tf_op jit(solution)/shard_map/ppermute | solution.py:212
  48.7 0.0 collective-permute-start.17
  48.7 0.4 shard_map.60
  49.1 2.0 %collective-permute-done.18.odd_in = f32[6,16,128]{2,1,0:T(8,128)S(1)} collective-permute-done((f32[6,16,128]{2,1,0:T(8,128)S(1)}, f32[6,16,128]{2,1,0:T(8,128)S(1)}, u32[]{:S(2)}, u32[]{:S(2)}) %collective-permute-start.18) | collective-permute-done | bytes 49184 | tf_op jit(solution)/shard_map/ppermute | solution.py:212
  51.0 0.0 collective-permute-done.17.even_in
  51.0 1.0 %shard_map.61 = f32[6,128,128]{2,1,0:T(8,128)} custom-call(f32[6,128,128]{2,1,0:T(8,128)S(1)} %get-tuple-element.65.inner, bf16[96,128]{1,0:T(8,128)(2,1)S(1)} %get-tuple-element.66.weights, f32[6,16,128]{2,1,0:T(8,128)S(1)} %collective-permute-done.17.even_in, f32[6,16,128]{2,1,0:T(8,128)S(1)} %collective-permute-done.18.odd_in), custom_call_target="tpu_custom_call" | custom-call | tf_op jit(solution)/shard_map/pallas_call | solution.py:224
  (13 shorter events, 0.3 us)
Async XLA Ops:
  0.7 9.0 %copy-start = (bf16[1,2,9,16,128,128]{5,4,3,2,1,0:T(8,128)(2,1)S(1)}, bf16[1,2,9,16,128,128]{5,4,3,2,1,0:T(8,128)(2,1)}, u32[]{:S(2)}) copy-start(bf16[1,2,9,16,128,128]{5,4,3,2,1,0:T(8,128)(2,1)} %refs_0_.5) | copy-start | bytes 28311556
  0.7 9.0 %copy-start.1 = (bf16[1,2,9,16,128,128]{5,4,3,2,1,0:T(8,128)(2,1)S(1)}, bf16[1,2,9,16,128,128]{5,4,3,2,1,0:T(8,128)(2,1)}, u32[]{:S(2)}) copy-start(bf16[1,2,9,16,128,128]{5,4,3,2,1,0:T(8,128)(2,1)} %refs_1_.5) | copy-start | bytes 28311556
  3.6 12.4 %collective-permute-start.1 = (f32[2,2,128,128]{3,2,1,0:T(8,128)S(1)}, f32[2,2,128,128]{3,2,1,0:T(8,128)S(1)}, u32[]{:S(2)}, u32[]{:S(2)}) collective-permute-start(f32[2,2,128,128]{3,2,1,0:T(8,128)S(1)} %get-tuple-element.43), channel_id=1, source_target_pairs={{0,16},{16,0},{32,48},{48,32},{64,80},{80,64},{96,112},{112,96},{1... | collective-permute-start | bytes 786440 | tf_op jit(solution)/shard_map/ppermute | solution.py:255
  6.2 11.2 %collective-permute-start.11 = (f32[2,2,128,128]{3,2,1,0:T(8,128)S(1)}, f32[2,2,128,128]{3,2,1,0:T(8,128)S(1)}, u32[]{:S(2)}, u32[]{:S(2)}) collective-permute-start(f32[2,2,128,128]{3,2,1,0:T(8,128)S(1)} %get-tuple-element.59), channel_id=1, source_target_pairs={{0,64},{16,80},{32,96},{48,112},{64,0},{80,16},{96,32},{112,48},{1... | collective-permute-start | bytes 786440 | tf_op jit(solution)/shard_map/ppermute | solution.py:255
  7.4 10.3 %collective-permute-start.6 = (f32[2,2,128,128]{3,2,1,0:T(8,128)S(1)}, f32[2,2,128,128]{3,2,1,0:T(8,128)S(1)}, u32[]{:S(2)}, u32[]{:S(2)}) collective-permute-start(f32[2,2,128,128]{3,2,1,0:T(8,128)S(1)} %get-tuple-element.51), channel_id=1, source_target_pairs={{0,48},{16,32},{32,16},{48,0},{64,112},{80,96},{96,80},{112,64},{1... | collective-permute-start | bytes 786440 | tf_op jit(solution)/shard_map/ppermute | solution.py:255
  11.1 17.2 %collective-permute-start.5 = (f32[2,2,128,128]{3,2,1,0:T(8,128)S(1)}, f32[2,2,128,128]{3,2,1,0:T(8,128)S(1)}, u32[]{:S(2)}, u32[]{:S(2)}) collective-permute-start(f32[2,2,128,128]{3,2,1,0:T(8,128)S(1)} %get-tuple-element.49), channel_id=1, source_target_pairs={{0,48},{16,32},{32,16},{48,0},{64,112},{80,96},{96,80},{112,64},{1... | collective-permute-start | bytes 786440 | tf_op jit(solution)/shard_map/ppermute | solution.py:255
  14.9 10.6 %collective-permute-start = (f32[2,2,128,128]{3,2,1,0:T(8,128)S(1)}, f32[2,2,128,128]{3,2,1,0:T(8,128)S(1)}, u32[]{:S(2)}, u32[]{:S(2)}) collective-permute-start(f32[2,2,128,128]{3,2,1,0:T(8,128)S(1)} %get-tuple-element.38), channel_id=1, source_target_pairs={{0,16},{16,0},{32,48},{48,32},{64,80},{80,64},{96,112},{112,96},{1... | collective-permute-start | bytes 786440 | tf_op jit(solution)/shard_map/ppermute | solution.py:255
  16.0 7.0 %collective-permute-start.10 = (f32[2,2,128,128]{3,2,1,0:T(8,128)S(1)}, f32[2,2,128,128]{3,2,1,0:T(8,128)S(1)}, u32[]{:S(2)}, u32[]{:S(2)}) collective-permute-start(f32[2,2,128,128]{3,2,1,0:T(8,128)S(1)} %get-tuple-element.57), channel_id=1, source_target_pairs={{0,64},{16,80},{32,96},{48,112},{64,0},{80,16},{96,32},{112,48},{1... | collective-permute-start | bytes 786440 | tf_op jit(solution)/shard_map/ppermute | solution.py:255
  17.4 8.6 %collective-permute-start.2 = (f32[2,128,128]{2,1,0:T(8,128)S(1)}, f32[2,128,128]{2,1,0:T(8,128)S(1)}, u32[]{:S(2)}, u32[]{:S(2)}) collective-permute-start(f32[2,128,128]{2,1,0:T(8,128)S(1)} %get-tuple-element.72), channel_id=1, source_target_pairs={{0,48},{16,32},{32,16},{48,0},{64,112},{80,96},{96,80},{112,64},{1... | collective-permute-start | bytes 393224 | tf_op jit(solution)/shard_map/ppermute | solution.py:255
  17.7 6.9 %collective-permute-start.12 = (f32[2,128,128]{2,1,0:T(8,128)S(1)}, f32[2,128,128]{2,1,0:T(8,128)S(1)}, u32[]{:S(2)}, u32[]{:S(2)}) collective-permute-start(f32[2,128,128]{2,1,0:T(8,128)S(1)} %get-tuple-element.76), channel_id=1, source_target_pairs={{0,16},{16,0},{32,48},{48,32},{64,80},{80,64},{96,112},{112,96},{1... | collective-permute-start | bytes 393224 | tf_op jit(solution)/shard_map/ppermute | solution.py:255
  23.0 6.0 %collective-permute-start.7 = (f32[2,128,128]{2,1,0:T(8,128)S(1)}, f32[2,128,128]{2,1,0:T(8,128)S(1)}, u32[]{:S(2)}, u32[]{:S(2)}) collective-permute-start(f32[2,128,128]{2,1,0:T(8,128)S(1)} %get-tuple-element.74), channel_id=1, source_target_pairs={{0,64},{16,80},{32,96},{48,112},{64,0},{80,16},{96,32},{112,48},{1... | collective-permute-start | bytes 393224 | tf_op jit(solution)/shard_map/ppermute | solution.py:255
  24.6 5.3 %collective-permute-start.13 = (f32[2,128,128]{2,1,0:T(8,128)S(1)}, f32[2,128,128]{2,1,0:T(8,128)S(1)}, u32[]{:S(2)}, u32[]{:S(2)}) collective-permute-start(f32[2,128,128]{2,1,0:T(8,128)S(1)} %get-tuple-element.75), channel_id=1, source_target_pairs={{0,16},{16,0},{32,48},{48,32},{64,80},{80,64},{96,112},{112,96},{1... | collective-permute-start | bytes 393224 | tf_op jit(solution)/shard_map/ppermute | solution.py:255
  25.5 5.1 %collective-permute-start.14 = (f32[2,128,128]{2,1,0:T(8,128)S(1)}, f32[2,128,128]{2,1,0:T(8,128)S(1)}, u32[]{:S(2)}, u32[]{:S(2)}) collective-permute-start(f32[2,128,128]{2,1,0:T(8,128)S(1)} %get-tuple-element.62), channel_id=1, source_target_pairs={{0,48},{16,32},{32,16},{48,0},{64,112},{80,96},{96,80},{112,64},{1... | collective-permute-start | bytes 393224 | tf_op jit(solution)/shard_map/ppermute | solution.py:255
  25.9 6.1 %collective-permute-start.3 = (f32[2,128,128]{2,1,0:T(8,128)S(1)}, f32[2,128,128]{2,1,0:T(8,128)S(1)}, u32[]{:S(2)}, u32[]{:S(2)}) collective-permute-start(f32[2,128,128]{2,1,0:T(8,128)S(1)} %get-tuple-element.71), channel_id=1, source_target_pairs={{0,48},{16,32},{32,16},{48,0},{64,112},{80,96},{96,80},{112,64},{1... | collective-permute-start | bytes 393224 | tf_op jit(solution)/shard_map/ppermute | solution.py:255
  28.3 5.6 %collective-permute-start.8 = (f32[2,128,128]{2,1,0:T(8,128)S(1)}, f32[2,128,128]{2,1,0:T(8,128)S(1)}, u32[]{:S(2)}, u32[]{:S(2)}) collective-permute-start(f32[2,128,128]{2,1,0:T(8,128)S(1)} %get-tuple-element.73), channel_id=1, source_target_pairs={{0,64},{16,80},{32,96},{48,112},{64,0},{80,16},{96,32},{112,48},{1... | collective-permute-start | bytes 393224 | tf_op jit(solution)/shard_map/ppermute | solution.py:255
  29.0 4.9 %collective-permute-start.4 = (f32[2,128,128]{2,1,0:T(8,128)S(1)}, f32[2,128,128]{2,1,0:T(8,128)S(1)}, u32[]{:S(2)}, u32[]{:S(2)}) collective-permute-start(f32[2,128,128]{2,1,0:T(8,128)S(1)} %get-tuple-element.46), channel_id=1, source_target_pairs={{0,64},{16,80},{32,96},{48,112},{64,0},{80,16},{96,32},{112,48},{1... | collective-permute-start | bytes 393224 | tf_op jit(solution)/shard_map/ppermute | solution.py:255
  29.9 4.2 %collective-permute-start.9 = (f32[2,128,128]{2,1,0:T(8,128)S(1)}, f32[2,128,128]{2,1,0:T(8,128)S(1)}, u32[]{:S(2)}, u32[]{:S(2)}) collective-permute-start(f32[2,128,128]{2,1,0:T(8,128)S(1)} %get-tuple-element.54), channel_id=1, source_target_pairs={{0,16},{16,0},{32,48},{48,32},{64,80},{80,64},{96,112},{112,96},{1... | collective-permute-start | bytes 393224 | tf_op jit(solution)/shard_map/ppermute | solution.py:255
  34.2 4.3 %collective-permute-start.16 = (f32[6,16,128]{2,1,0:T(8,128)S(1)}, f32[6,16,128]{2,1,0:T(8,128)S(1)}, u32[]{:S(2)}, u32[]{:S(2)}) collective-permute-start(f32[6,16,128]{2,1,0:T(8,128)S(1)} %get-tuple-element.69), channel_id=1, source_target_pairs={{0,12},{4,8},{8,4},{12,0},{1,13},{5,9},{9,5},{13,1},{2,14},{6,10},... | collective-permute-start | bytes 147464 | tf_op jit(solution)/shard_map/ppermute | solution.py:212
  37.0 2.9 %collective-permute-start.15 = (f32[6,16,128]{2,1,0:T(8,128)S(1)}, f32[6,16,128]{2,1,0:T(8,128)S(1)}, u32[]{:S(2)}, u32[]{:S(2)}) collective-permute-start(f32[6,16,128]{2,1,0:T(8,128)S(1)} %get-tuple-element.70), channel_id=1, source_target_pairs={{0,4},{4,0},{8,12},{12,8},{1,5},{5,1},{9,13},{13,9},{2,6},{6,2},{1... | collective-permute-start | bytes 147464 | tf_op jit(solution)/shard_map/ppermute | solution.py:211
  40.2 10.8 %collective-permute-start.18 = (f32[6,16,128]{2,1,0:T(8,128)S(1)}, f32[6,16,128]{2,1,0:T(8,128)S(1)}, u32[]{:S(2)}, u32[]{:S(2)}) collective-permute-start(f32[6,16,128]{2,1,0:T(8,128)S(1)} %get-tuple-element.67), channel_id=1, source_target_pairs={{0,3},{1,2},{2,1},{3,0},{4,7},{5,6},{6,5},{7,4},{8,11},{9,10},{10,... | collective-permute-start | bytes 147464 | tf_op jit(solution)/shard_map/ppermute | solution.py:212
  48.7 2.4 %collective-permute-start.17 = (f32[6,16,128]{2,1,0:T(8,128)S(1)}, f32[6,16,128]{2,1,0:T(8,128)S(1)}, u32[]{:S(2)}, u32[]{:S(2)}) collective-permute-start(f32[6,16,128]{2,1,0:T(8,128)S(1)} %get-tuple-element.68), channel_id=1, source_target_pairs={{0,1},{1,0},{2,3},{3,2},{4,5},{5,4},{6,7},{7,6},{8,9},{9,8},{10,11... | collective-permute-start | bytes 147464 | tf_op jit(solution)/shard_map/ppermute | solution.py:211

commit v4 on v3

--- a/solution.py
+++ b/solution.py
@@ -272,18 +272,17 @@
     density11 = swap(v["density11"], "x")
     v |= gradient(
         (forward, adjoint, v["taper"], v["factors"]),
-        (True, True),
+        (True, False),
         [
-            (3, 6, (0, 0, 1), (("lame01_0", 0), ("shear10", 0))),
+            (3, 6, (0, 0, 1), (None, ("shear10", 0))),
             (3, 6, (0, 1, 1), (None, ("shear10", 1))),
-            (3, 6, (0, 1, 0), (("lame10", 0), ("shear00_1", 0))),
-            (3, 6, (1, 1, 0), (("lame10", 1), ("shear01_1", 0))),
+            (3, 3, (0, 1, 0), (("lame10", 0), None)),
+            (3, 3, (1, 1, 0), (("lame10", 1), None)),
             (0, 3, (1, 0, 0), (("density10", 0),)),
             (0, 3, (1, 0, 1), (("density10", 1),)),
         ],
         {
             "lame10": 2, "shear10": 2, "density10": 2,
-            "lame01_0": 1, "shear00_1": 1, "shear01_1": 1,
         },
     )
     shear10 = swap(v["shear10"], "b")
@@ -294,6 +293,9 @@
         (forward, adjoint, taper, v["factors"]),
         (True, True),
         [
+            (3, 3, (0, 0, 1), (("lame01_0", 0), None)),
+            (3, 6, (0, 1, 0), (None, ("shear00_1", 0))),
+            (3, 6, (1, 1, 0), (None, ("shear01_1", 0))),
             (3, 6, (1, 0, 0), (("lame00_1", 0), ("shear01_0", 0))),
             (0, 3, (0, 1, 0), (("density01_0", 0),)),
             (0, 3, (0, 1, 1), (("density01_1", 0),)),
@@ -302,7 +304,8 @@
             (0, 3, (0, 0, 1), (("density00_1", 0),)),
         ],
         {
-            "lame00_0": 1, "lame00_1": 1, "shear00_0": 1, "shear01_0": 1,
+            "lame00_0": 1, "lame00_1": 1, "lame01_0": 1,
+            "shear00_0": 1, "shear00_1": 1, "shear01_0": 1, "shear01_1": 1,
             "density00_0": 1, "density00_1": 1, "density01_0": 1, "density01_1": 1,
         },
     )

time: 52.1 us -> 52.5 us (level)
  starting transfers between devices: 30.4 us -> 28.8 us
  Pallas kernels: 7.75 us -> 9.31 us
    ppermute x15, starting transfers between devices: 19.1 us -> 17 us  [swap(): return lax.ppermute(v, 'shot', [(i, i ^ flips[dim]) for i in range(shots)])]
    pallas_call x3, Pallas kernels: 5.61 us -> 7.16 us  [gradient(): pl.pallas_call(functools.partial(gradient_kernel, steps, len(names), resi...]
  transfers between devices with their start and end apart: 19 -> 19, of which waited for: 9 -> 7; matrix products, arithmetic and copies ran while one was open for 0% -> 0% of each run, Pallas kernels for 7% -> 10%
where the time goes in v4:
time: 52.5 us; the launch traced here: 52.4 us
  starting transfers between devices  28.8 us (55%)
  waiting for transfers between devices  13.2 us (25%)
  Pallas kernels  9.31 us (18%)
  between operations  0.87 us (2%)
    ppermute x15, starting transfers between devices, swap(): return lax.ppermute(v, 'shot', [(i, i ^ flips[dim]) for i in range(shots)])  17 us
    ppermute x2, starting transfers between devices, smooth(): second = lax.ppermute(jnp.where(even, head, tail), axis, swaps[1])  11.7 us
    ppermute x15, waiting for transfers between devices, swap(): return lax.ppermute(v, 'shot', [(i, i ^ flips[dim]) for i in range(shots)])  8.62 us
    pallas_call x3, Pallas kernels, gradient(): pl.pallas_call(functools.partial(gradient_kernel, steps, len(names), resi...  7.16 us
    ppermute x2, waiting for transfers between devices, smooth(): second = lax.ppermute(jnp.where(even, head, tail), axis, swaps[1])  3.14 us
    ppermute x2, waiting for transfers between devices, smooth(): first = lax.ppermute(jnp.where(even, tail, head), axis, swaps[0])  1.46 us
    pallas_call x2, Pallas kernels, smooth(): pl.pallas_call(outer_kernel, out_shape=(jax.ShapeDtypeStruct if last else...  1.22 us
  transfers between devices with their start and end apart: 19, of which 7 were waited for; matrix products, arithmetic and copies ran while one was open for 0% of the time, Pallas kernels for 10%

profile of v4, /device:TPU:1, one launch (start us, length us, event | category | flops | bytes accessed | tf_op | source)
XLA Modules:
  0.0 52.4 jit_solution(5745491299846079627)
XLA Ops:
  0.7 0.0 slice-start
  0.7 0.0 slice-start.1
  0.7 3.0 %shard_map.55 = (f32[2,2,128,128]{3,2,1,0:T(8,128)S(1)}, f32[2,2,128,128]{3,2,1,0:T(8,128)S(1)}, f32[2,2,128,128]{3,2,1,0:T(8,128)S(1)}, f32[1,2,128,128]{3,2,1,...) custom-call(bf16[1,2,9,16,128,128]{5,4,3,2,1,0:T(8,128)(2,1)} %refs_0_.5, ...), custom_call_target="tpu_custom_call" | custom-call | tf_op jit(solution)/shard_map/pallas_call | solution.py:136
  3.7 2.1 %collective-permute-start.11 = (f32[2,2,128,128]{3,2,1,0:T(8,128)S(1)}, f32[2,2,128,128]{3,2,1,0:T(8,128)S(1)}, u32[]{:S(2)}, u32[]{:S(2)}) collective-permute-start(f32[2,2,128,128]{3,2,1,0:T(8,128)S(1)} %get-tuple-element.59), channel_id=1, source_target_pairs={{0,64},{16,80},{32,96},{48,112},{64,0},{80,16},{96,32},{112,48},{1... | collective-permute-start | bytes 786440 | tf_op jit(solution)/shard_map/ppermute | solution.py:255
  5.8 3.8 %collective-permute-start.6 = (f32[2,2,128,128]{3,2,1,0:T(8,128)S(1)}, f32[2,2,128,128]{3,2,1,0:T(8,128)S(1)}, u32[]{:S(2)}, u32[]{:S(2)}) collective-permute-start(f32[2,2,128,128]{3,2,1,0:T(8,128)S(1)} %get-tuple-element.51), channel_id=1, source_target_pairs={{0,48},{16,32},{32,16},{48,0},{64,112},{80,96},{96,80},{112,64},{1... | collective-permute-start | bytes 786440 | tf_op jit(solution)/shard_map/ppermute | solution.py:255
  9.5 0.0 collective-permute-start.1
  9.5 0.0 copy-done
  9.5 2.3 %shard_map.56 = (f32[2,2,128,128]{3,2,1,0:T(8,128)S(1)}, f32[2,2,128,128]{3,2,1,0:T(8,128)S(1)}, f32[2,2,128,128]{3,2,1,0:T(8,128)S(1)}) custom-call(bf16[1,2,9,16,128,128]{5,4,3,2,1,0:T(8,128)(2,1)S(1)} %copy-done, bf16[1,2,9,16,128,128]{5,4,3,2,1,0:T(8,128)(2,1)} %refs_1_.5, f32[128,128]{1,0:T(8,128)S(1)} %get-tuple-element.39.refs_2_, ...), custom_call_target="tpu_custom_call" | custom-call | tf_op jit(solution)/shard_map/pallas_call | solution.py:136
  11.9 1.5 %collective-permute-start.5 = (f32[2,2,128,128]{3,2,1,0:T(8,128)S(1)}, f32[2,2,128,128]{3,2,1,0:T(8,128)S(1)}, u32[]{:S(2)}, u32[]{:S(2)}) collective-permute-start(f32[2,2,128,128]{3,2,1,0:T(8,128)S(1)} %get-tuple-element.49), channel_id=1, source_target_pairs={{0,48},{16,32},{32,16},{48,0},{64,112},{80,96},{96,80},{112,64},{1... | collective-permute-start | bytes 786440 | tf_op jit(solution)/shard_map/ppermute | solution.py:255
  13.4 0.1 collective-permute-start
  13.5 1.9 %shard_map.57 = (f32[1,2,128,128]{3,2,1,0:T(8,128)S(1)}, f32[1,2,128,128]{3,2,1,0:T(8,128)S(1)}, f32[1,2,128,128]{3,2,1,0:T(8,128)S(1)}, f32[1,2,128,128]{3,2,1,...) custom-call(bf16[1,2,9,16,128,128]{5,4,3,2,1,0:T(8,128)(2,1)S(1)} %c, ...), custom_call_target="tpu_custom_call" | custom-call | tf_op jit(solution)/shard_map/pallas_call | solution.py:136
  15.4 0.0 collective-permute-done.11
  15.4 1.2 %collective-permute-start.10 = (f32[2,2,128,128]{3,2,1,0:T(8,128)S(1)}, f32[2,2,128,128]{3,2,1,0:T(8,128)S(1)}, u32[]{:S(2)}, u32[]{:S(2)}) collective-permute-start(f32[2,2,128,128]{3,2,1,0:T(8,128)S(1)} %get-tuple-element.57), channel_id=1, source_target_pairs={{0,64},{16,80},{32,96},{48,112},{64,0},{80,16},{96,32},{112,48},{1... | collective-permute-start | bytes 786440 | tf_op jit(solution)/shard_map/ppermute | solution.py:255
  16.6 0.0 collective-permute-done.6
  16.6 1.5 %collective-permute-start.12 = (f32[2,128,128]{2,1,0:T(8,128)S(1)}, f32[2,128,128]{2,1,0:T(8,128)S(1)}, u32[]{:S(2)}, u32[]{:S(2)}) collective-permute-start(f32[2,128,128]{2,1,0:T(8,128)S(1)} %get-tuple-element.76), channel_id=1, source_target_pairs={{0,16},{16,0},{32,48},{48,32},{64,80},{80,64},{96,112},{112,96},{1... | collective-permute-start | bytes 393224 | tf_op jit(solution)/shard_map/ppermute | solution.py:255
  18.2 0.0 collective-permute-done.1
  18.2 0.3 collective-permute-start.7
  18.5 3.0 %collective-permute-done.10.in10 = f32[2,2,128,128]{3,2,1,0:T(8,128)S(1)} collective-permute-done((f32[2,2,128,128]{3,2,1,0:T(8,128)S(1)}, f32[2,2,128,128]{3,2,1,0:T(8,128)S(1)}, u32[]{:S(2)}, u32[]{:S(2)}) %collective-permute-start.10) | collective-permute-done | bytes 262176 | tf_op jit(solution)/shard_map/ppermute | solution.py:255
  21.5 1.7 %collective-permute-start.2 = (f32[2,128,128]{2,1,0:T(8,128)S(1)}, f32[2,128,128]{2,1,0:T(8,128)S(1)}, u32[]{:S(2)}, u32[]{:S(2)}) collective-permute-start(f32[2,128,128]{2,1,0:T(8,128)S(1)} %get-tuple-element.72), channel_id=1, source_target_pairs={{0,48},{16,32},{32,16},{48,0},{64,112},{80,96},{96,80},{112,64},{1... | collective-permute-start | bytes 393224 | tf_op jit(solution)/shard_map/ppermute | solution.py:255
  23.2 1.3 %collective-permute-done.12.in01_1 = f32[2,128,128]{2,1,0:T(8,128)S(1)} collective-permute-done((f32[2,128,128]{2,1,0:T(8,128)S(1)}, f32[2,128,128]{2,1,0:T(8,128)S(1)}, u32[]{:S(2)}, u32[]{:S(2)}) %collective-permute-start.12) | collective-permute-done | bytes 131104 | tf_op jit(solution)/shard_map/ppermute | solution.py:255
  24.6 0.3 collective-permute-start.13
  24.9 0.0 collective-permute-done.5.in10
  24.9 0.7 %collective-permute-start.14 = (f32[2,128,128]{2,1,0:T(8,128)S(1)}, f32[2,128,128]{2,1,0:T(8,128)S(1)}, u32[]{:S(2)}, u32[]{:S(2)}) collective-permute-start(f32[2,128,128]{2,1,0:T(8,128)S(1)} %get-tuple-element.62), channel_id=1, source_target_pairs={{0,48},{16,32},{32,16},{48,0},{64,112},{80,96},{96,80},{112,64},{1... | collective-permute-start | bytes 393224 | tf_op jit(solution)/shard_map/ppermute | solution.py:255
  25.6 0.0 collective-permute-done.7.in01_1
  25.6 1.2 %collective-permute-start.8 = (f32[2,128,128]{2,1,0:T(8,128)S(1)}, f32[2,128,128]{2,1,0:T(8,128)S(1)}, u32[]{:S(2)}, u32[]{:S(2)}) collective-permute-start(f32[2,128,128]{2,1,0:T(8,128)S(1)} %get-tuple-element.73), channel_id=1, source_target_pairs={{0,64},{16,80},{32,96},{48,112},{64,0},{80,16},{96,32},{112,48},{1... | collective-permute-start | bytes 393224 | tf_op jit(solution)/shard_map/ppermute | solution.py:255
  26.9 0.0 collective-permute-done.in10
  26.9 1.8 %collective-permute-start.3 = (f32[2,128,128]{2,1,0:T(8,128)S(1)}, f32[2,128,128]{2,1,0:T(8,128)S(1)}, u32[]{:S(2)}, u32[]{:S(2)}) collective-permute-start(f32[2,128,128]{2,1,0:T(8,128)S(1)} %get-tuple-element.71), channel_id=1, source_target_pairs={{0,48},{16,32},{32,16},{48,0},{64,112},{80,96},{96,80},{112,64},{1... | collective-permute-start | bytes 393224 | tf_op jit(solution)/shard_map/ppermute | solution.py:255
  28.7 0.0 collective-permute-done.2.in01_1
  28.7 0.3 collective-permute-start.9
  29.0 0.0 collective-permute-done.13
  29.0 0.6 %collective-permute-start.4 = (f32[2,128,128]{2,1,0:T(8,128)S(1)}, f32[2,128,128]{2,1,0:T(8,128)S(1)}, u32[]{:S(2)}, u32[]{:S(2)}) collective-permute-start(f32[2,128,128]{2,1,0:T(8,128)S(1)} %get-tuple-element.46), channel_id=1, source_target_pairs={{0,64},{16,80},{32,96},{48,112},{64,0},{80,16},{96,32},{112,48},{1... | collective-permute-start | bytes 393224 | tf_op jit(solution)/shard_map/ppermute | solution.py:255
  29.5 1.1 %collective-permute-done.14 = f32[2,128,128]{2,1,0:T(8,128)S(1)} collective-permute-done((f32[2,128,128]{2,1,0:T(8,128)S(1)}, f32[2,128,128]{2,1,0:T(8,128)S(1)}, u32[]{:S(2)}, u32[]{:S(2)}) %collective-permute-start.14) | collective-permute-done | bytes 131104 | tf_op jit(solution)/shard_map/ppermute | solution.py:255
  30.7 0.0 collective-permute-done.8
  30.7 3.1 %collective-permute-done.9 = f32[2,128,128]{2,1,0:T(8,128)S(1)} collective-permute-done((f32[2,128,128]{2,1,0:T(8,128)S(1)}, f32[2,128,128]{2,1,0:T(8,128)S(1)}, u32[]{:S(2)}, u32[]{:S(2)}) %collective-permute-start.9) | collective-permute-done | bytes 131104 | tf_op jit(solution)/shard_map/ppermute | solution.py:255
  33.9 0.0 collective-permute-done.3
  33.9 0.0 collective-permute-done.4
  34.0 2.8 %collective-permute-start.16 = (f32[6,16,128]{2,1,0:T(8,128)S(1)}, f32[6,16,128]{2,1,0:T(8,128)S(1)}, u32[]{:S(2)}, u32[]{:S(2)}) collective-permute-start(f32[6,16,128]{2,1,0:T(8,128)S(1)} %get-tuple-element.69), channel_id=1, source_target_pairs={{0,12},{4,8},{8,4},{12,0},{1,13},{5,9},{9,5},{13,1},{2,14},{6,10},... | collective-permute-start | bytes 147464 | tf_op jit(solution)/shard_map/ppermute | solution.py:212
  36.8 0.0 collective-permute-start.15
  36.8 0.4 shard_map.58
  37.2 1.1 %collective-permute-done.16.odd_in = f32[6,16,128]{2,1,0:T(8,128)S(1)} collective-permute-done((f32[6,16,128]{2,1,0:T(8,128)S(1)}, f32[6,16,128]{2,1,0:T(8,128)S(1)}, u32[]{:S(2)}, u32[]{:S(2)}) %collective-permute-start.16) | collective-permute-done | bytes 49184 | tf_op jit(solution)/shard_map/ppermute | solution.py:212
  38.3 1.5 %collective-permute-done.15.even_in = f32[6,16,128]{2,1,0:T(8,128)S(1)} collective-permute-done((f32[6,16,128]{2,1,0:T(8,128)S(1)}, f32[6,16,128]{2,1,0:T(8,128)S(1)}, u32[]{:S(2)}, u32[]{:S(2)}) %collective-permute-start.15) | collective-permute-done | bytes 49184 | tf_op jit(solution)/shard_map/ppermute | solution.py:211
  39.7 0.2 shard_map.59.cells
  40.0 8.9 %collective-permute-start.18 = (f32[6,16,128]{2,1,0:T(8,128)S(1)}, f32[6,16,128]{2,1,0:T(8,128)S(1)}, u32[]{:S(2)}, u32[]{:S(2)}) collective-permute-start(f32[6,16,128]{2,1,0:T(8,128)S(1)} %get-tuple-element.67), channel_id=1, source_target_pairs={{0,3},{1,2},{2,1},{3,0},{4,7},{5,6},{6,5},{7,4},{8,11},{9,10},{10,... | collective-permute-start | bytes 147464 | tf_op jit(solution)/shard_map/ppermute | solution.py:212
  48.9 0.0 collective-permute-start.17
  48.9 0.4 shard_map.60
  49.3 2.1 %collective-permute-done.18.odd_in = f32[6,16,128]{2,1,0:T(8,128)S(1)} collective-permute-done((f32[6,16,128]{2,1,0:T(8,128)S(1)}, f32[6,16,128]{2,1,0:T(8,128)S(1)}, u32[]{:S(2)}, u32[]{:S(2)}) %collective-permute-start.18) | collective-permute-done | bytes 49184 | tf_op jit(solution)/shard_map/ppermute | solution.py:212
  51.4 0.0 collective-permute-done.17.even_in
  51.4 1.0 %shard_map.61 = f32[6,128,128]{2,1,0:T(8,128)} custom-call(f32[6,128,128]{2,1,0:T(8,128)S(1)} %get-tuple-element.65.inner, bf16[96,128]{1,0:T(8,128)(2,1)S(1)} %get-tuple-element.66.weights, f32[6,16,128]{2,1,0:T(8,128)S(1)} %collective-permute-done.17.even_in, f32[6,16,128]{2,1,0:T(8,128)S(1)} %collective-permute-done.18.odd_in), custom_call_target="tpu_custom_call" | custom-call | tf_op jit(solution)/shard_map/pallas_call | solution.py:224
  (18 shorter events, 0.3 us)
Async XLA Ops:
  0.7 8.9 %copy-start = (bf16[1,2,9,16,128,128]{5,4,3,2,1,0:T(8,128)(2,1)S(1)}, bf16[1,2,9,16,128,128]{5,4,3,2,1,0:T(8,128)(2,1)}, u32[]{:S(2)}) copy-start(bf16[1,2,9,16,128,128]{5,4,3,2,1,0:T(8,128)(2,1)} %refs_0_.5) | copy-start | bytes 28311556
  0.7 12.8 %slice-start = ((s8[9437184]{0:T(1024)(128)(4,1)}), s8[1048576]{0:T(1024)(128)(4,1)S(1)}, s32[]{:S(2)}) async-start(s8[9437184]{0:T(1024)(128)(4,1)} %bitcast.13), calls=%async_computation | async-start | bytes 2097152
  0.7 12.8 %slice-start.1 = ((s8[9437184]{0:T(1024)(128)(4,1)}), s8[4194304]{0:T(1024)(128)(4,1)S(1)}, s32[]{:S(2)}) async-start(s8[9437184]{0:T(1024)(128)(4,1)} %bitcast.13), calls=%async_computation.1 | async-start | bytes 8388608
  3.7 11.7 %collective-permute-start.11 = (f32[2,2,128,128]{3,2,1,0:T(8,128)S(1)}, f32[2,2,128,128]{3,2,1,0:T(8,128)S(1)}, u32[]{:S(2)}, u32[]{:S(2)}) collective-permute-start(f32[2,2,128,128]{3,2,1,0:T(8,128)S(1)} %get-tuple-element.59), channel_id=1, source_target_pairs={{0,64},{16,80},{32,96},{48,112},{64,0},{80,16},{96,32},{112,48},{1... | collective-permute-start | bytes 786440 | tf_op jit(solution)/shard_map/ppermute | solution.py:255
  5.8 10.8 %collective-permute-start.6 = (f32[2,2,128,128]{3,2,1,0:T(8,128)S(1)}, f32[2,2,128,128]{3,2,1,0:T(8,128)S(1)}, u32[]{:S(2)}, u32[]{:S(2)}) collective-permute-start(f32[2,2,128,128]{3,2,1,0:T(8,128)S(1)} %get-tuple-element.51), channel_id=1, source_target_pairs={{0,48},{16,32},{32,16},{48,0},{64,112},{80,96},{96,80},{112,64},{1... | collective-permute-start | bytes 786440 | tf_op jit(solution)/shard_map/ppermute | solution.py:255
  9.5 8.7 %collective-permute-start.1 = (f32[2,2,128,128]{3,2,1,0:T(8,128)S(1)}, f32[2,2,128,128]{3,2,1,0:T(8,128)S(1)}, u32[]{:S(2)}, u32[]{:S(2)}) collective-permute-start(f32[2,2,128,128]{3,2,1,0:T(8,128)S(1)} %get-tuple-element.43), channel_id=1, source_target_pairs={{0,16},{16,0},{32,48},{48,32},{64,80},{80,64},{96,112},{112,96},{1... | collective-permute-start | bytes 786440 | tf_op jit(solution)/shard_map/ppermute | solution.py:255
  9.5 4.0 %slice-start.2 = ((s8[9437184]{0:T(1024)(128)(4,1)}), s8[4194304]{0:T(1024)(128)(4,1)S(1)}, s32[]{:S(2)}) async-start(s8[9437184]{0:T(1024)(128)(4,1)} %bitcast.13), calls=%async_computation.2 | async-start | bytes 8388608
  11.9 13.0 %collective-permute-start.5 = (f32[2,2,128,128]{3,2,1,0:T(8,128)S(1)}, f32[2,2,128,128]{3,2,1,0:T(8,128)S(1)}, u32[]{:S(2)}, u32[]{:S(2)}) collective-permute-start(f32[2,2,128,128]{3,2,1,0:T(8,128)S(1)} %get-tuple-element.49), channel_id=1, source_target_pairs={{0,48},{16,32},{32,16},{48,0},{64,112},{80,96},{96,80},{112,64},{1... | collective-permute-start | bytes 786440 | tf_op jit(solution)/shard_map/ppermute | solution.py:255
  13.4 13.5 %collective-permute-start = (f32[2,2,128,128]{3,2,1,0:T(8,128)S(1)}, f32[2,2,128,128]{3,2,1,0:T(8,128)S(1)}, u32[]{:S(2)}, u32[]{:S(2)}) collective-permute-start(f32[2,2,128,128]{3,2,1,0:T(8,128)S(1)} %get-tuple-element.38), channel_id=1, source_target_pairs={{0,16},{16,0},{32,48},{48,32},{64,80},{80,64},{96,112},{112,96},{1... | collective-permute-start | bytes 786440 | tf_op jit(solution)/shard_map/ppermute | solution.py:255
  15.4 6.1 %collective-permute-start.10 = (f32[2,2,128,128]{3,2,1,0:T(8,128)S(1)}, f32[2,2,128,128]{3,2,1,0:T(8,128)S(1)}, u32[]{:S(2)}, u32[]{:S(2)}) collective-permute-start(f32[2,2,128,128]{3,2,1,0:T(8,128)S(1)} %get-tuple-element.57), channel_id=1, source_target_pairs={{0,64},{16,80},{32,96},{48,112},{64,0},{80,16},{96,32},{112,48},{1... | collective-permute-start | bytes 786440 | tf_op jit(solution)/shard_map/ppermute | solution.py:255
  16.6 8.0 %collective-permute-start.12 = (f32[2,128,128]{2,1,0:T(8,128)S(1)}, f32[2,128,128]{2,1,0:T(8,128)S(1)}, u32[]{:S(2)}, u32[]{:S(2)}) collective-permute-start(f32[2,128,128]{2,1,0:T(8,128)S(1)} %get-tuple-element.76), channel_id=1, source_target_pairs={{0,16},{16,0},{32,48},{48,32},{64,80},{80,64},{96,112},{112,96},{1... | collective-permute-start | bytes 393224 | tf_op jit(solution)/shard_map/ppermute | solution.py:255
  18.2 7.5 %collective-permute-start.7 = (f32[2,128,128]{2,1,0:T(8,128)S(1)}, f32[2,128,128]{2,1,0:T(8,128)S(1)}, u32[]{:S(2)}, u32[]{:S(2)}) collective-permute-start(f32[2,128,128]{2,1,0:T(8,128)S(1)} %get-tuple-element.74), channel_id=1, source_target_pairs={{0,64},{16,80},{32,96},{48,112},{64,0},{80,16},{96,32},{112,48},{1... | collective-permute-start | bytes 393224 | tf_op jit(solution)/shard_map/ppermute | solution.py:255
  21.5 7.1 %collective-permute-start.2 = (f32[2,128,128]{2,1,0:T(8,128)S(1)}, f32[2,128,128]{2,1,0:T(8,128)S(1)}, u32[]{:S(2)}, u32[]{:S(2)}) collective-permute-start(f32[2,128,128]{2,1,0:T(8,128)S(1)} %get-tuple-element.72), channel_id=1, source_target_pairs={{0,48},{16,32},{32,16},{48,0},{64,112},{80,96},{96,80},{112,64},{1... | collective-permute-start | bytes 393224 | tf_op jit(solution)/shard_map/ppermute | solution.py:255
  24.6 4.4 %collective-permute-start.13 = (f32[2,128,128]{2,1,0:T(8,128)S(1)}, f32[2,128,128]{2,1,0:T(8,128)S(1)}, u32[]{:S(2)}, u32[]{:S(2)}) collective-permute-start(f32[2,128,128]{2,1,0:T(8,128)S(1)} %get-tuple-element.75), channel_id=1, source_target_pairs={{0,16},{16,0},{32,48},{48,32},{64,80},{80,64},{96,112},{112,96},{1... | collective-permute-start | bytes 393224 | tf_op jit(solution)/shard_map/ppermute | solution.py:255
  24.9 5.7 %collective-permute-start.14 = (f32[2,128,128]{2,1,0:T(8,128)S(1)}, f32[2,128,128]{2,1,0:T(8,128)S(1)}, u32[]{:S(2)}, u32[]{:S(2)}) collective-permute-start(f32[2,128,128]{2,1,0:T(8,128)S(1)} %get-tuple-element.62), channel_id=1, source_target_pairs={{0,48},{16,32},{32,16},{48,0},{64,112},{80,96},{96,80},{112,64},{1... | collective-permute-start | bytes 393224 | tf_op jit(solution)/shard_map/ppermute | solution.py:255
  25.6 5.0 %collective-permute-start.8 = (f32[2,128,128]{2,1,0:T(8,128)S(1)}, f32[2,128,128]{2,1,0:T(8,128)S(1)}, u32[]{:S(2)}, u32[]{:S(2)}) collective-permute-start(f32[2,128,128]{2,1,0:T(8,128)S(1)} %get-tuple-element.73), channel_id=1, source_target_pairs={{0,64},{16,80},{32,96},{48,112},{64,0},{80,16},{96,32},{112,48},{1... | collective-permute-start | bytes 393224 | tf_op jit(solution)/shard_map/ppermute | solution.py:255
  26.9 7.0 %collective-permute-start.3 = (f32[2,128,128]{2,1,0:T(8,128)S(1)}, f32[2,128,128]{2,1,0:T(8,128)S(1)}, u32[]{:S(2)}, u32[]{:S(2)}) collective-permute-start(f32[2,128,128]{2,1,0:T(8,128)S(1)} %get-tuple-element.71), channel_id=1, source_target_pairs={{0,48},{16,32},{32,16},{48,0},{64,112},{80,96},{96,80},{112,64},{1... | collective-permute-start | bytes 393224 | tf_op jit(solution)/shard_map/ppermute | solution.py:255
  28.7 5.2 %collective-permute-start.9 = (f32[2,128,128]{2,1,0:T(8,128)S(1)}, f32[2,128,128]{2,1,0:T(8,128)S(1)}, u32[]{:S(2)}, u32[]{:S(2)}) collective-permute-start(f32[2,128,128]{2,1,0:T(8,128)S(1)} %get-tuple-element.54), channel_id=1, source_target_pairs={{0,16},{16,0},{32,48},{48,32},{64,80},{80,64},{96,112},{112,96},{1... | collective-permute-start | bytes 393224 | tf_op jit(solution)/shard_map/ppermute | solution.py:255
  29.0 4.9 %collective-permute-start.4 = (f32[2,128,128]{2,1,0:T(8,128)S(1)}, f32[2,128,128]{2,1,0:T(8,128)S(1)}, u32[]{:S(2)}, u32[]{:S(2)}) collective-permute-start(f32[2,128,128]{2,1,0:T(8,128)S(1)} %get-tuple-element.46), channel_id=1, source_target_pairs={{0,64},{16,80},{32,96},{48,112},{64,0},{80,16},{96,32},{112,48},{1... | collective-permute-start | bytes 393224 | tf_op jit(solution)/shard_map/ppermute | solution.py:255
  34.0 4.3 %collective-permute-start.16 = (f32[6,16,128]{2,1,0:T(8,128)S(1)}, f32[6,16,128]{2,1,0:T(8,128)S(1)}, u32[]{:S(2)}, u32[]{:S(2)}) collective-permute-start(f32[6,16,128]{2,1,0:T(8,128)S(1)} %get-tuple-element.69), channel_id=1, source_target_pairs={{0,12},{4,8},{8,4},{12,0},{1,13},{5,9},{9,5},{13,1},{2,14},{6,10},... | collective-permute-start | bytes 147464 | tf_op jit(solution)/shard_map/ppermute | solution.py:212
  36.8 2.9 %collective-permute-start.15 = (f32[6,16,128]{2,1,0:T(8,128)S(1)}, f32[6,16,128]{2,1,0:T(8,128)S(1)}, u32[]{:S(2)}, u32[]{:S(2)}) collective-permute-start(f32[6,16,128]{2,1,0:T(8,128)S(1)} %get-tuple-element.70), channel_id=1, source_target_pairs={{0,4},{4,0},{8,12},{12,8},{1,5},{5,1},{9,13},{13,9},{2,6},{6,2},{1... | collective-permute-start | bytes 147464 | tf_op jit(solution)/shard_map/ppermute | solution.py:211
  40.0 11.4 %collective-permute-start.18 = (f32[6,16,128]{2,1,0:T(8,128)S(1)}, f32[6,16,128]{2,1,0:T(8,128)S(1)}, u32[]{:S(2)}, u32[]{:S(2)}) collective-permute-start(f32[6,16,128]{2,1,0:T(8,128)S(1)} %get-tuple-element.67), channel_id=1, source_target_pairs={{0,3},{1,2},{2,1},{3,0},{4,7},{5,6},{6,5},{7,4},{8,11},{9,10},{10,... | collective-permute-start | bytes 147464 | tf_op jit(solution)/shard_map/ppermute | solution.py:212
  48.9 2.5 %collective-permute-start.17 = (f32[6,16,128]{2,1,0:T(8,128)S(1)}, f32[6,16,128]{2,1,0:T(8,128)S(1)}, u32[]{:S(2)}, u32[]{:S(2)}) collective-permute-start(f32[6,16,128]{2,1,0:T(8,128)S(1)} %get-tuple-element.68), channel_id=1, source_target_pairs={{0,1},{1,0},{2,3},{3,2},{4,5},{5,4},{6,7},{7,6},{8,9},{9,8},{10,11... | collective-permute-start | bytes 147464 | tf_op jit(solution)/shard_map/ppermute | solution.py:211
